TPU v7x, 32 devices: a whole 2x2x4 slice. The times are simulated.
32 devices in a mesh: gx: 4 (over z), gy: 4 (over x, core), gz: 2 (over y).
Axes of the slice: x: 2, y: 2, z: 4, core: 2. Of those that a mesh axis runs over, the one named last changes fastest.
Arguments:
- coords: float32 [3, 4, 1024, 128], P(None, 'gx', ('gy', 'gz')), may hold values from 0 to 11
- charges: float32 [4, 1024, 128], P('gx', ('gy', 'gz')), may hold values from -1.5 to 1.5
- atom_types: int32 [4, 1024, 128], P('gx', ('gy', 'gz')), may hold values from 0 to 63
- lj_sigma: float32 [64], replicated, may hold values from 2 to 4
- lj_epsilon: float32 [64], replicated, may hold values from 0.02 to 0.25
- tile_list: int32 [4, 4, 2, 2, 512], P('gx', 'gy', 'gz'), may hold values from -1 to 3455, as said below
Outputs:
- forces: float32 [3, 4, 1024, 128], P(None, 'gx', ('gy', 'gz'))
Inputs may be any that keep to these rules, and one draw needn't show every extreme that they name: tile_list[x, y, z, 0, t] is a block of brick (x, y, z) (0 to 127) and tile_list[x, y, z, 1, t] a block of its neighbourhood whose cell touches the home block's cell or is that cell (cell indices differ by at most one along each dimension, counted across brick faces periodically); on each brick the listed tiles come first and the remaining slots hold -1 in both rows; at least 256 tiles are listed on every brick and all 512 on some brick; tiles may repeat.
All inputs are finite; a program needn't handle non-finite values.
Results may differ from a plain program's by a relative error of at most 0.0003.
Values sent between devices are 32-bit elements; how exact they have to be, the bound alone decides.
A program may use at most 128 MiB of HBM per device.

v0:
```python
import itertools
import math

import jax
import jax.numpy as jnp
from jax import lax
from jax.experimental import pallas as pl
from jax.experimental.pallas import tpu as pltpu
from jax.sharding import PartitionSpec as P

GRID = 4
ROWS = 8
BATCH = 8

cell_edge = 11.0
cutoff = 9.0
soft_core = 16.0
coulomb = 332.0636
limit = cutoff * cutoff + soft_core
sigma_scale = 0.5 * 2.0 ** (1.0 / 6.0)
charge_scale = (coulomb / 12.0) ** 0.5


def exchange_kernel(atoms, region, send_own, recv_own, send_rim, recv_rim, own_sem):
    stride, ranks = atoms.shape[:2]
    layers = region.shape[2] - 2
    spans = [lax.axis_size(name) for name in ("gx", "gy", "gz")]
    here = [lax.axis_index(name) for name in ("gx", "gy", "gz")]
    me = here[1] * spans[2] + here[2]
    chunk = math.gcd(stride, layers)
    pieces = stride // chunk

    def place(piece):
        cell = me * stride + piece * chunk
        return region.at[
            cell // (GRID * layers) + 1,
            lax.rem(cell // layers, GRID) + 1,
            pl.ds(lax.rem(cell, layers) + 1, chunk),
        ]

    copies = []
    for hop in range(1, ranks):
        to = lax.rem(me + hop, ranks)
        for piece in range(pieces):
            sem = (hop - 1) * pieces + piece
            copies.append(
                pltpu.make_async_remote_copy(
                    src_ref=atoms.at[pl.ds(piece * chunk, chunk), to],
                    dst_ref=place(piece),
                    send_sem=send_own.at[sem],
                    recv_sem=recv_own.at[sem],
                    device_id=(here[0], to // spans[2], lax.rem(to, spans[2])),
                    device_id_type=pl.DeviceIdType.MESH,
                )
            )
            copies[-1].start()
    for piece in range(pieces):
        kept = pltpu.make_async_copy(
            atoms.at[pl.ds(piece * chunk, chunk), me], place(piece), own_sem.at[piece]
        )
        kept.start()
        copies.append(kept)
    for copy in copies:
        copy.wait()

    lengths = (GRID, GRID, layers)
    rims = []
    offsets = [o for o in itertools.product((-1, 0, 1), repeat=3) if any(o)]
    for sem, offset in enumerate(offsets):
        source = tuple(
            pl.ds(1, n) if o == 0 else pl.ds(n if o > 0 else 1, 1)
            for o, n in zip(offset, lengths)
        )
        target = tuple(
            pl.ds(1, n) if o == 0 else pl.ds(0 if o > 0 else n + 1, 1)
            for o, n in zip(offset, lengths)
        )
        rims.append(
            pltpu.make_async_remote_copy(
                src_ref=region.at[source],
                dst_ref=region.at[target],
                send_sem=send_rim.at[sem],
                recv_sem=recv_rim.at[sem],
                device_id=tuple(
                    lax.rem(at + o + n, n) for at, o, n in zip(here, offset, spans)
                ),
                device_id_type=pl.DeviceIdType.MESH,
            )
        )
        rims[-1].start()
    for copy in rims:
        copy.wait()


def exchanged(atoms, layers):
    stride, ranks, rows, width = atoms.shape
    pieces = stride // math.gcd(stride, layers)
    own = pltpu.SemaphoreType.DMA(((ranks - 1) * pieces,))
    rim = pltpu.SemaphoreType.DMA((26,))
    return pl.pallas_call(
        exchange_kernel,
        out_shape=jax.ShapeDtypeStruct(
            (GRID + 2, GRID + 2, layers + 2, rows, width), atoms.dtype
        ),
        in_specs=[pl.BlockSpec(memory_space=pltpu.VMEM)],
        out_specs=pl.BlockSpec(memory_space=pltpu.VMEM),
        scratch_shapes=[own, own, rim, rim, pltpu.SemaphoreType.DMA((pieces,))],
        compiler_params=pltpu.CompilerParams(has_side_effects=True),
    )(atoms)


def split(value):
    high = value.astype(jnp.bfloat16).astype(jnp.float32)
    rest = value - high
    middle = rest.astype(jnp.bfloat16).astype(jnp.float32)
    return high, middle, rest - middle


def stacked(parts):
    return jnp.concatenate(parts, axis=0).astype(jnp.bfloat16)


def quotient(value, size):
    if size & (size - 1):
        return lax.div(value, size)
    return lax.shift_right_logical(value, size.bit_length() - 1)


def remainder(value, size):
    if size & (size - 1):
        return lax.rem(value, size)
    return value & (size - 1)


def rows_of(shape):
    return lax.broadcasted_iota(jnp.int32, shape, 0)


def row_table(values, shape):
    rows = rows_of(shape)
    out = jnp.zeros(shape, jnp.float32)
    for k, value in enumerate(values):
        if value:
            out = jnp.where(rows == k, jnp.float32(value), out)
    return out


def rising_powers(base, rows):
    two = base * base
    four = two * two
    out = jnp.where(rows % 2 == 1, base, 1.0)
    out = out * jnp.where(rows // 2 % 2 == 1, two, 1.0)
    return out * jnp.where(rows // 4 % 2 == 1, four, 1.0)


def prepare_sources(region, sources, weights, moments):
    shape = region.shape[1:]
    rows = rows_of(shape)
    count = moments.shape[2]
    ways = row_table([math.comb(6, k) for k in range(7)], shape)
    edge = 1.0 / limit
    high_at = row_table([edge**7 * math.comb(12, k) for k in range(7)], shape)
    low_at = row_table([-(edge**4) * math.comb(6, k) for k in range(7)], shape)
    wide_at = row_table([0.0] + [edge**7 * math.comb(12, k + 6) for k in range(1, 7)], shape)
    near_at = jnp.where(rows == 7, inverse_powers(jnp.full(shape, limit, jnp.float32))[1], 0.0)
    lanes = lax.broadcasted_iota(jnp.int32, (ROWS, count), 1)
    kept = (rows_of((ROWS, count)) >= 4) == (lanes % (2 * ROWS) == 7)

    def one(line, carry):
        block = region[line]
        high, middle, low = split(block)
        sigma = jnp.broadcast_to(region[line, 5:6, :], shape)
        root = jnp.broadcast_to(region[line, 6:7, :], shape)
        charge = jnp.broadcast_to(region[line, 7:8, :], shape)
        falling = rising_powers(sigma, 6 - jnp.minimum(rows, 6))
        square = sigma * sigma
        top, rest, _ = split(ways * falling)
        sources[line] = stacked([high, middle, high, middle, high, low, top, rest, top, rest])
        place = jnp.where(rows < 4, block, pltpu.roll(block, 4, 0))
        top, rest, _ = split(place * jnp.where(rows < 4, root, charge))
        left = stacked([top, rest])
        weights[line] = left
        first = split(falling * (high_at * (square * square * square) + low_at) + near_at)
        second = split(falling * wide_at)
        both = lax.dot_general(
            left,
            stacked([first[0], second[0], first[1], second[1]]),
            (((1,), (1,)), ((), ())),
            preferred_element_type=jnp.float32,
        )
        moments[line] = jnp.where(kept, both[:ROWS] + both[ROWS:], 0.0)
        return carry

    lax.fori_loop(0, region.shape[0], one, 0, unroll=4)


def prepare_homes(region, distances, powers, scales, layers):
    shape = region.shape[1:]
    rows = rows_of(shape)
    blocks = distances.shape[0] - 1

    def one(block, carry):
        line = own_line(block, layers)
        home = region[line]
        distances[block] = jnp.where(rows < 3, -2.0 * home, jnp.where(rows == 4, 1.0, 0.0))
        top, rest, _ = split(rising_powers(jnp.broadcast_to(region[line, 5:6, :], shape), rows))
        powers[block] = stacked([top, top, rest, rest])
        root = jnp.broadcast_to(region[line, 6:7, :], shape)
        charge = jnp.broadcast_to(region[line, 7:8, :], shape)
        scales[block] = 12.0 * jnp.where(rows < 4, root, charge)
        return carry

    lax.fori_loop(0, blocks, one, 0, unroll=4)
    distances[blocks] = jnp.zeros(shape, jnp.float32)
    powers[blocks] = jnp.zeros(powers.shape[1:], powers.dtype)


def own_line(block, layers):
    x = quotient(block, GRID * layers)
    y = remainder(quotient(block, layers), GRID)
    return ((x + 1) * (GRID + 2) + y + 1) * (layers + 2) + remainder(block, layers) + 1


def prepare_steps(offsets, shifts):
    shape = offsets.shape[1:]
    for step, cells in enumerate(itertools.product((-1, 0, 1), repeat=3)):
        moves = [cell_edge * c for c in cells]
        offsets[step] = row_table([2.0 * m for m in moves], shape)
        shifts[step] = row_table(moves + [0.0] + moves, shape)


def pair_terms(pairs, index, sources, distances, powers, offsets, terms):
    home = pairs[0, index]
    distance = distances[home] + offsets[pairs[2, index]]
    rows = rows_of(distance.shape)
    share = jnp.where(rows < 3, 0.25, jnp.where(rows == 4, soft_core, 0.0))
    square = jnp.sum(distance * distance * share, axis=0, keepdims=True)
    distance = jnp.where(rows == 3, square, distance)
    high, middle, low = split(distance)
    near = stacked([high, high, middle, middle, low, high])
    strong = powers[home]
    width = near.shape[1]
    right = jnp.concatenate(
        [
            jnp.concatenate([near, jnp.zeros((strong.shape[0], width), near.dtype)], axis=0),
            jnp.concatenate([jnp.zeros(near.shape, near.dtype), strong], axis=0),
        ],
        axis=1,
    )
    terms[...] = lax.dot_general(
        sources[pairs[1, index]],
        right,
        (((0,), (0,)), ((), ())),
        preferred_element_type=jnp.float32,
    )


def inverse_powers(softened):
    root = lax.rsqrt(softened)
    one = root * root
    return one, one * root


def strengths(terms, nears, strongs):
    width = terms.shape[0]
    for start in range(0, width, 16):
        rows = pl.ds(start, 16)
        one, near = inverse_powers(jnp.minimum(terms[rows, :width], limit))
        sixth = terms[rows, width:] * (near * near)
        for halves, value in ((nears, near), (strongs, one * (sixth * (sixth - 1.0)))):
            top = value.astype(jnp.bfloat16)
            halves[rows, :] = top
            halves[pl.ds(width + start, 16), :] = (value - top.astype(jnp.float32)).astype(jnp.bfloat16)


def add_forces(pairs, index, weights, moments, shifts, nears, strongs, totals, edges):
    line = pairs[1, index]
    left = weights[line]
    both = jnp.dot(
        jnp.concatenate([left, left], axis=1),
        jnp.concatenate([nears[...], strongs[...]], axis=1),
        preferred_element_type=jnp.float32,
    )
    both = both[:ROWS] + both[ROWS:]
    width = left.shape[1]
    rows = rows_of((ROWS, width))
    summed = jnp.where(rows < 4, both[:, width:], both[:, :width])
    plain = jnp.where(rows < 4, summed[3:4], summed[7:8])
    shift = shifts[pairs[2, index]]
    home = pairs[0, index]
    totals[home] += summed + shift * plain
    shape = moments.shape[1:]
    count = shape[1]
    plain = jnp.where(
        rows[:, :count] < 4,
        jnp.broadcast_to(moments[line, 3:4, :], shape),
        jnp.broadcast_to(moments[line, 7:8, :], shape),
    )
    edges[home] += moments[line] + shift[:, :count] * plain


def force_kernel(
    pairs, count, region, out, totals, sources, weights, moments, distances, powers, scales, edges, offsets, shifts, *slots
):
    blocks = out.shape[1]
    layers = blocks // (GRID * GRID)
    totals[...] = jnp.zeros_like(totals)
    edges[...] = jnp.zeros_like(edges)
    prepare_steps(offsets, shifts)
    prepare_sources(region, sources, weights, moments)
    prepare_homes(region, distances, powers, scales, layers)
    terms, nears, strongs = [
        (slots[k : k + BATCH], slots[k + BATCH : k + 2 * BATCH]) for k in range(0, 6 * BATCH, 2 * BATCH)
    ]

    def step(index, carry):
        for turn in range(2):
            first = (2 * index + turn) * BATCH
            for t in range(BATCH):
                add_forces(
                    pairs, first + t, weights, moments, shifts, nears[turn][t], strongs[turn][t], totals, edges
                )
                strengths(terms[1 - turn][t], nears[1 - turn][t], strongs[1 - turn][t])
                pair_terms(pairs, first + 2 * BATCH + t, sources, distances, powers, offsets, terms[turn][t])
        return carry

    groups = (count[0] + BATCH - 1) // BATCH
    lax.fori_loop(0, (groups + 3) // 2, step, 0)

    def finish(block, carry):
        home = region[own_line(block, layers)]
        rows = rows_of(home.shape)
        place = jnp.where(rows < 4, home, pltpu.roll(home, 4, 0))
        sigma = jnp.broadcast_to(home[5:6], home.shape)
        rising = rising_powers(sigma, rows)
        square = sigma * sigma
        first = split(jnp.where(rows == 7, 1.0, rising))
        second = split(rising * (square * square * square))
        right = stacked([first[0], second[0], first[0], second[0], first[1], second[1], first[1], second[1]])
        edge = edges[block]
        left = stacked([*split(edge), jnp.zeros_like(edge)])
        both = jnp.dot(jnp.concatenate([left, left], axis=1), right, preferred_element_type=jnp.float32)
        summed = totals[block] - (both[:ROWS] + both[ROWS : 2 * ROWS] + both[2 * ROWS : 3 * ROWS])
        plain = jnp.where(rows < 4, summed[3:4], summed[7:8])
        force = (place * plain - summed) * scales[block]
        totals[block] = force + pltpu.roll(force, 4, 0)
        return carry

    lax.fori_loop(0, blocks, finish, 0, unroll=4)
    for axis in range(3):
        out[axis] = totals[:blocks, axis, :]


def brick_forces(region, pairs, count, blocks):
    lines, _, width = region.shape
    single = pltpu.VMEM((blocks + 1, ROWS, width), jnp.float32)
    table = pltpu.VMEM((27, ROWS, width), jnp.float32)
    return pl.pallas_call(
        force_kernel,
        out_shape=jax.ShapeDtypeStruct((3, blocks, width), jnp.float32),
        in_specs=[
            pl.BlockSpec(memory_space=pltpu.SMEM),
            pl.BlockSpec(memory_space=pltpu.SMEM),
            pl.BlockSpec(memory_space=pltpu.VMEM),
        ],
        out_specs=pl.BlockSpec(memory_space=pltpu.VMEM),
        scratch_shapes=[
            single,
            pltpu.VMEM((lines, 10 * ROWS, width), jnp.bfloat16),
            pltpu.VMEM((lines, 2 * ROWS, width), jnp.bfloat16),
            pltpu.VMEM((lines, ROWS, 4 * ROWS), jnp.float32),
            single,
            pltpu.VMEM((blocks + 1, 4 * ROWS, width), jnp.bfloat16),
            single,
            pltpu.VMEM((blocks + 1, ROWS, 4 * ROWS), jnp.float32),
            table,
            table,
        ]
        + [pltpu.VMEM((width, 2 * width), jnp.float32)] * (2 * BATCH)
        + [pltpu.VMEM((2 * width, width), jnp.bfloat16)] * (4 * BATCH),
    )(pairs, count, region)


def per_device(coords, charges, atom_types, lj_sigma, lj_epsilon, tile_list):
    span_y = lax.axis_size("gy")
    span_z = lax.axis_size("gz")
    blocks = coords.shape[2]
    width = coords.shape[3]
    layers = blocks // (GRID * GRID)
    ranks = span_y * span_z
    stride = blocks // ranks
    dtype = coords.dtype
    kinds = jnp.arange(lj_sigma.shape[0], dtype=jnp.int32)
    selector = (atom_types[0][:, :, None] == kinds).astype(dtype)
    sigma_atom = jnp.sum(selector * (lj_sigma * sigma_scale), axis=2)
    root_atom = jnp.sum(selector * (jnp.sqrt(lj_epsilon)), axis=2)
    inner = coords[:, 0] - 0.5 * cell_edge
    square = inner[0] * inner[0] + inner[1] * inner[1] + inner[2] * inner[2]
    atoms = jnp.stack(
        [inner[0], inner[1], inner[2], jnp.ones_like(square), square]
        + [sigma_atom, root_atom, charges[0] * charge_scale],
        axis=1,
    )
    outgoing = atoms.reshape(stride, ranks, ROWS, width)
    padded = exchanged(outgoing, layers)
    region = padded.reshape(-1, ROWS, width)
    pairs = jnp.pad(
        tile_list[0, 0, 0], ((0, 0), (2 * BATCH, 4 * BATCH)), constant_values=-1
    )
    dead = pairs[0] < 0

    def place(ids):
        slot = ids // blocks
        member = ids % blocks
        px = member // (GRID * layers) + (slot // 9 - 1) * GRID
        py = member // layers % GRID + (slot // 3 % 3 - 1) * GRID
        pz = member % layers + (slot % 3 - 1) * layers
        return px, py, pz

    own = place(jnp.where(dead, 0, pairs[0]) + 13 * blocks)
    other = place(jnp.where(dead, 13 * blocks, pairs[1]))
    x, y, z = other
    line = ((x + 1) * (GRID + 2) + y + 1) * (layers + 2) + z + 1
    dx, dy, dz = [b - a + 1 for a, b in zip(own, other)]
    table = jnp.stack([jnp.where(dead, blocks, pairs[0]), line, (dx * 3 + dy) * 3 + dz])
    count = jnp.sum((~dead).astype(jnp.int32)).reshape(1)
    totals = brick_forces(region, table, count, blocks)
    sending = totals.reshape(3, ranks, stride, width)[:, :, :, None]
    returned = lax.all_to_all(sending, ("gy", "gz"), split_axis=1, concat_axis=3, tiled=True)
    return returned.reshape(3, 1, blocks, width)


def solution(mesh):
    return jax.shard_map(
        per_device,
        mesh=mesh,
        in_specs=(
            P(None, "gx", ("gy", "gz"), None),
            P("gx", ("gy", "gz"), None),
            P("gx", ("gy", "gz"), None),
            P(),
            P(),
            P("gx", "gy", "gz", None, None),
        ),
        out_specs=P(None, "gx", ("gy", "gz"), None),
        check_vma=False,
    )
```

profile of v0, /device:TPU:0, one launch (start us, length us, event | category | flops | bytes accessed | tf_op | source)
XLA Modules:
  0.0 111.8 jit_solution(7974966578694015418)
XLA Ops:
  0.0 0.7 broadcast_multiply_fusion.1
  0.7 0.7 sqrt.3
  1.3 0.9 and_select_fusion.19
  2.2 0.8 broadcast_multiply_fusion
  3.0 0.9 broadcast_add_fusion
  4.0 2.9 %select_reduce_fusion = (f32[128,128]{1,0:T(8,128)S(1)}, f32[128,128]{1,0:T(8,128)S(1)}) fusion(f32[64]{0:T(128)S(1)} %sqrt.3, s32[128,128]{1,0:T(8,128)} %bitcast.36, f32[64]{0:T(128)S(1)} %broadcast_multiply_fusion.1), kind=kLoop, calls=%fused_computation | loop fusion | flops 5210112 | bytes 197120 | tf_op jit(solution)/shard_map/reduce_sum | solution.py:396
  7.0 0.0 copy-start
  7.0 1.5 %stack.29.atoms = f32[16,8,8,128]{3,2,1,0:T(8,128)} concatenate(f32[16,8,1,128]{3,2,1,0:T(1,128)S(1)} %bitcast.31, f32[16,8,1,128]{3,2,1,0:T(1,128)S(1)} %bitcast.29, f32[16,8,1,128]{3,2,1,0:T(1,128)S(1)} %bitcast.27, f32[16,8,1,128]{3,2,1,0:T(1,128)S(1)} %stack_broadcast_in_dim.3, f32[16,8,1,128]{3,2,1,0:T(1,128)S(1)} %bitcast.35, f32[16,8,1,128]{3,2,1,0:T(1,128)S(1)} %bitcast.33, ...), dimensions={2} | concatenate | bytes 1048576 | tf_op jit(solution)/shard_map/stack | solution.py:399
  8.4 33.8 %shard_map.64 = f32[6,6,10,8,128]{4,3,2,1,0:T(8,128)} custom-call(f32[16,8,8,128]{3,2,1,0:T(8,128)} %stack.29.atoms), custom_call_target="tpu_custom_call" | custom-call | tf_op jit(solution)/shard_map/pallas_call | solution.py:100
  42.3 0.1 add_add_fusion.1
  42.4 0.0 copy-done
  42.4 0.8 fusion.17
  43.2 0.6 pad_add_fusion.pairs
  43.8 53.2 %shard_map.65 = f32[3,128,128]{2,1,0:T(8,128)} custom-call(s32[3,560]{1,0:T(4,128)} %pad_add_fusion.pairs, s32[1]{0:T(128)} %bitcast.1.count, f32[360,8,128]{2,1,0:T(8,128)} %bitcast.24), custom_call_target="tpu_custom_call" | custom-call | tf_op jit(solution)/shard_map/pallas_call | solution.py:358
  97.0 0.9 copy.12
  97.9 13.1 %all_to_all.15 = f32[3,8,16,1,128]{4,2,0,3,1:T(8,128)S(1)} all-to-all(f32[3,8,16,1,128]{4,2,0,3,1:T(8,128)S(1)} %copy.12), channel_id=1, replica_groups=mesh['gx'=4,'gy'=4,'gz'=2] {'gy','gz'}, dimensions={1} | all-to-all | bytes 393216 | tf_op jit(solution)/shard_map/all_to_all | solution.py:429
  111.0 0.7 copy.16
  (3 shorter events, 0.1 us)
Async XLA Ops:
  7.0 35.4 %copy-start = (s32[1,1,1,2,512]{4,3,2,1,0:T(2,128)S(1)}, s32[1,1,1,2,512]{4,3,2,1,0:T(2,128)}, u32[]{:S(2)}) copy-start(s32[1,1,1,2,512]{4,3,2,1,0:T(2,128)} %param.11) | copy-start | bytes 12292
where the time goes:
time: 113 us; the launch traced here: 112 us
  Pallas kernels  87 us (77%)
  blocking collectives  13.1 us (12%)
  other arithmetic  7.69 us (7%)
  local copies, waits for them, and re-layouts  3.87 us (3%)
    pallas_call x1, Pallas kernels, brick_forces(): pl.pallas_call(force_kernel, out_shape=jax.ShapeDtypeStruct((3, blocks, w...  53.2 us
    pallas_call x1, Pallas kernels, exchanged(): pl.pallas_call(exchange_kernel, out_shape=jax.ShapeDtypeStruct((GRID + 2,...  33.8 us
    all_to_all x1, blocking collectives, per_device(): lax.all_to_all(sending, ('gy', 'gz'), split_axis=1, concat_axis=3, tiled=...  13.1 us
    reduce_sum x1, other arithmetic, per_device(): root_atom = jnp.sum(selector * jnp.sqrt(lj_epsilon), axis=2)  2.89 us

commit v1 on v0

--- a/solution.py
+++ b/solution.py
@@ -10,7 +10,8 @@
 
 GRID = 4
 ROWS = 8
-BATCH = 8
+BATCH = 4
+EDGE = 128
 
 cell_edge = 11.0
 cutoff = 9.0
@@ -21,26 +22,108 @@
 charge_scale = (coulomb / 12.0) ** 0.5
 
 
-def exchange_kernel(atoms, region, send_own, recv_own, send_rim, recv_rim, own_sem):
+def spans_of():
+    names = ("gx", "gy", "gz")
+    return [lax.axis_size(n) for n in names], [lax.axis_index(n) for n in names]
+
+
+def plane_peers(spans, here):
+    ranks = spans[1] * spans[2]
+    me = here[1] * spans[2] + here[2]
+    for hop in range(1, ranks):
+        to = lax.rem(me + hop, ranks)
+        yield hop, to, (here[0], quotient(to, spans[2]), remainder(to, spans[2]))
+
+
+def brick_neighbours(spans, here):
+    for offset in itertools.product((-1, 0, 1), repeat=3):
+        if any(offset):
+            yield offset, tuple(lax.rem(at + o + n, n) for at, o, n in zip(here, offset, spans))
+
+
+def greet(devices):
+    barrier = pltpu.get_barrier_semaphore()
+    for device in devices:
+        pl.semaphore_signal(barrier, inc=1, device_id=device, device_id_type=pl.DeviceIdType.MESH)
+    return barrier, len(devices)
+
+
+def looked_up(values, kinds):
+    padded = jnp.concatenate([values, jnp.zeros((1, kinds.shape[1] - values.shape[1]), values.dtype)], axis=1)
+    return jnp.take_along_axis(jnp.broadcast_to(padded, kinds.shape), kinds, axis=1)
+
+
+def pack_atoms(coords, charges, kinds, sigma, epsilon, atoms):
+    stride, ranks = atoms.shape[:2]
+    sigmas = sigma[...] * sigma_scale
+    roots = jnp.sqrt(epsilon[...])
+    for group in range(stride):
+        rows = pl.ds(group * ranks, ranks)
+        inner = [coords[axis, rows, :] - 0.5 * cell_edge for axis in range(3)]
+        kind = kinds[rows, :]
+        square = inner[0] * inner[0] + inner[1] * inner[1] + inner[2] * inner[2]
+        values = inner + [jnp.ones_like(square), square, looked_up(sigmas, kind), looked_up(roots, kind)]
+        values.append(charges[rows, :] * charge_scale)
+        for row, value in enumerate(values):
+            atoms[group, :, row, :] = value
+
+
+def cell_of(member, layers):
+    return (
+        quotient(member, GRID * layers),
+        remainder(quotient(member, layers), GRID),
+        remainder(member, layers),
+    )
+
+
+def thirds(value, size):
+    return sum((value >= k * size).astype(jnp.int32) for k in (1, 2))
+
+
+def tile_table(tiles, table, blocks, layers):
+    home, other = tiles[0:1, :], tiles[1:2, :]
+    dead = home < 0
+    slot = quotient(jnp.where(dead, 13 * blocks, other), blocks)
+    member = remainder(jnp.where(dead, 0, other), blocks)
+    far = thirds(slot, 9)
+    slot = slot - 9 * far
+    middle = thirds(slot, 3)
+    steps = (far - 1, middle - 1, slot - 3 * middle - 1)
+    sizes = (GRID, GRID, layers)
+    own = cell_of(jnp.where(dead, 0, home), layers)
+    there = [c + s * n for c, s, n in zip(cell_of(member, layers), steps, sizes)]
+    line = ((there[0] + 1) * (GRID + 2) + there[1] + 1) * (layers + 2) + there[2] + 1
+    delta = [t - o + 1 for t, o in zip(there, own)]
+    width = tiles.shape[1]
+    table[...] = jnp.where(rows_of(table.shape) == 0, blocks, 0)
+    table[0:1, EDGE : EDGE + width] = jnp.where(dead, blocks, home)
+    table[1:2, EDGE : EDGE + width] = line
+    table[2:3, EDGE : EDGE + width] = (delta[0] * 3 + delta[1]) * 3 + delta[2]
+
+
+def exchange_kernel(
+    coords, charges, kinds, sigma, epsilon, tiles, region, table, atoms, send_own, recv_own, send_rim, recv_rim, own_sem
+):
     stride, ranks = atoms.shape[:2]
     layers = region.shape[2] - 2
-    spans = [lax.axis_size(name) for name in ("gx", "gy", "gz")]
-    here = [lax.axis_index(name) for name in ("gx", "gy", "gz")]
+    blocks = stride * ranks
+    spans, here = spans_of()
     me = here[1] * spans[2] + here[2]
+    peers = list(plane_peers(spans, here))
+    neighbours = list(brick_neighbours(spans, here))
+    barrier, greeted = greet([p[2] for p in peers] + [n[1] for n in neighbours])
+    pack_atoms(coords, charges, kinds, sigma, epsilon, atoms)
+    tile_table(tiles, table, blocks, layers)
+    pl.semaphore_wait(barrier, greeted)
     chunk = math.gcd(stride, layers)
     pieces = stride // chunk
 
     def place(piece):
-        cell = me * stride + piece * chunk
-        return region.at[
-            cell // (GRID * layers) + 1,
-            lax.rem(cell // layers, GRID) + 1,
-            pl.ds(lax.rem(cell, layers) + 1, chunk),
-        ]
+        x, y, z = cell_of(me * stride + piece * chunk, layers)
+        return region.at[x + 1, y + 1, pl.ds(z + 1, chunk)]
 
     copies = []
-    for hop in range(1, ranks):
-        to = lax.rem(me + hop, ranks)
+    for hop, to, device in peers:
         for piece in range(pieces):
             sem = (hop - 1) * pieces + piece
             copies.append(
@@ -49,7 +132,7 @@
                     dst_ref=place(piece),
                     send_sem=send_own.at[sem],
                     recv_sem=recv_own.at[sem],
-                    device_id=(here[0], to // spans[2], lax.rem(to, spans[2])),
+                    device_id=device,
                     device_id_type=pl.DeviceIdType.MESH,
                 )
             )
@@ -65,8 +148,7 @@
 
     lengths = (GRID, GRID, layers)
     rims = []
-    offsets = [o for o in itertools.product((-1, 0, 1), repeat=3) if any(o)]
-    for sem, offset in enumerate(offsets):
+    for sem, (offset, device) in enumerate(neighbours):
         source = tuple(
             pl.ds(1, n) if o == 0 else pl.ds(n if o > 0 else 1, 1)
             for o, n in zip(offset, lengths)
@@ -81,9 +163,7 @@
                 dst_ref=region.at[target],
                 send_sem=send_rim.at[sem],
                 recv_sem=recv_rim.at[sem],
-                device_id=tuple(
-                    lax.rem(at + o + n, n) for at, o, n in zip(here, offset, spans)
-                ),
+                device_id=device,
                 device_id_type=pl.DeviceIdType.MESH,
             )
         )
@@ -92,21 +172,77 @@
         copy.wait()
 
 
-def exchanged(atoms, layers):
-    stride, ranks, rows, width = atoms.shape
+def exchanged(coords, charges, kinds, sigma, epsilon, tiles, ranks):
+    blocks, width = charges.shape
+    layers = blocks // (GRID * GRID)
+    stride = blocks // ranks
     pieces = stride // math.gcd(stride, layers)
     own = pltpu.SemaphoreType.DMA(((ranks - 1) * pieces,))
     rim = pltpu.SemaphoreType.DMA((26,))
+    vmem = pl.BlockSpec(memory_space=pltpu.VMEM)
     return pl.pallas_call(
         exchange_kernel,
-        out_shape=jax.ShapeDtypeStruct(
-            (GRID + 2, GRID + 2, layers + 2, rows, width), atoms.dtype
+        out_shape=(
+            jax.ShapeDtypeStruct((GRID + 2, GRID + 2, layers + 2, ROWS, width), coords.dtype),
+            jax.ShapeDtypeStruct((ROWS, tiles.shape[1] + 2 * EDGE), jnp.int32),
         ),
-        in_specs=[pl.BlockSpec(memory_space=pltpu.VMEM)],
-        out_specs=pl.BlockSpec(memory_space=pltpu.VMEM),
-        scratch_shapes=[own, own, rim, rim, pltpu.SemaphoreType.DMA((pieces,))],
-        compiler_params=pltpu.CompilerParams(has_side_effects=True),
-    )(atoms)
+        in_specs=[vmem] * 6,
+        out_specs=(vmem, vmem),
+        scratch_shapes=[
+            pltpu.VMEM((stride, ranks, ROWS, width), coords.dtype),
+            own,
+            own,
+            rim,
+            rim,
+            pltpu.SemaphoreType.DMA((pieces,)),
+        ],
+        compiler_params=pltpu.CompilerParams(
+            has_side_effects=True, collective_id=0, vmem_limit_bytes=8 << 20
+        ),
+    )(coords, charges, kinds, sigma, epsilon, tiles)
+
+
+def return_kernel(forces, out, send, recv, own_sem):
+    spans, here = spans_of()
+    me = here[1] * spans[2] + here[2]
+    peers = list(plane_peers(spans, here))
+    barrier, greeted = greet([p[2] for p in peers])
+    kept = pltpu.make_async_copy(forces.at[:, me], out.at[:, :, me], own_sem.at[0])
+    kept.start()
+    pl.semaphore_wait(barrier, greeted)
+    copies = [kept]
+    for hop, to, device in peers:
+        copies.append(
+            pltpu.make_async_remote_copy(
+                src_ref=forces.at[:, to],
+                dst_ref=out.at[:, :, me],
+                send_sem=send.at[hop - 1],
+                recv_sem=recv.at[hop - 1],
+                device_id=device,
+                device_id_type=pl.DeviceIdType.MESH,
+            )
+        )
+        copies[-1].start()
+    for copy in copies:
+        copy.wait()
+
+
+def returned(forces, ranks):
+    axes, blocks, width = forces.shape
+    stride = blocks // ranks
+    sems = pltpu.SemaphoreType.DMA((ranks - 1,))
+    vmem = pl.BlockSpec(memory_space=pltpu.VMEM)
+    out = pl.pallas_call(
+        return_kernel,
+        out_shape=jax.ShapeDtypeStruct((axes, stride, ranks, 1, width), forces.dtype),
+        in_specs=[vmem],
+        out_specs=vmem,
+        scratch_shapes=[sems, sems, pltpu.SemaphoreType.DMA((1,))],
+        compiler_params=pltpu.CompilerParams(
+            has_side_effects=True, collective_id=1, vmem_limit_bytes=4 << 20
+        ),
+    )(forces.reshape(axes, ranks, stride, 1, width))
+    return out.reshape(axes, 1, blocks, width)
 
 
 def split(value):
@@ -153,7 +289,7 @@
     return out * jnp.where(rows // 4 % 2 == 1, four, 1.0)
 
 
-def prepare_sources(region, sources, weights, moments):
+def prepare_sources(region, sources, weights, moments, edge_terms):
     shape = region.shape[1:]
     rows = rows_of(shape)
     count = moments.shape[2]
@@ -166,7 +302,7 @@
     lanes = lax.broadcasted_iota(jnp.int32, (ROWS, count), 1)
     kept = (rows_of((ROWS, count)) >= 4) == (lanes % (2 * ROWS) == 7)
 
-    def one(line, carry):
+    def spread(line):
         block = region[line]
         high, middle, low = split(block)
         sigma = jnp.broadcast_to(region[line, 5:6, :], shape)
@@ -178,20 +314,35 @@
         sources[line] = stacked([high, middle, high, middle, high, low, top, rest, top, rest])
         place = jnp.where(rows < 4, block, pltpu.roll(block, 4, 0))
         top, rest, _ = split(place * jnp.where(rows < 4, root, charge))
-        left = stacked([top, rest])
-        weights[line] = left
+        weights[line] = stacked([top, rest])
         first = split(falling * (high_at * (square * square * square) + low_at) + near_at)
         second = split(falling * wide_at)
+        edge_terms[line] = stacked([first[0], second[0], first[1], second[1]])
+
+    def summed(line):
         both = lax.dot_general(
-            left,
-            stacked([first[0], second[0], first[1], second[1]]),
+            weights[line],
+            edge_terms[line],
             (((1,), (1,)), ((), ())),
             preferred_element_type=jnp.float32,
         )
         moments[line] = jnp.where(kept, both[:ROWS] + both[ROWS:], 0.0)
+
+    lines = region.shape[0]
+    group = max(n for n in range(1, 25) if lines % n == 0)
+
+    def one(index, carry):
+        for k in range(group):
+            summed((index - 1) * group + k)
+        for k in range(group):
+            spread(index * group + k)
         return carry
 
-    lax.fori_loop(0, region.shape[0], one, 0, unroll=4)
+    for k in range(group):
+        spread(k)
+    lax.fori_loop(1, lines // group, one, 0)
+    for k in range(group):
+        summed(lines - group + k)
 
 
 def prepare_homes(region, distances, powers, scales, layers):
@@ -300,14 +451,14 @@
 
 
 def force_kernel(
-    pairs, count, region, out, totals, sources, weights, moments, distances, powers, scales, edges, offsets, shifts, *slots
+    pairs, region, out, totals, sources, weights, moments, distances, powers, scales, edges, edge_terms, offsets, shifts, *slots
 ):
     blocks = out.shape[1]
     layers = blocks // (GRID * GRID)
     totals[...] = jnp.zeros_like(totals)
     edges[...] = jnp.zeros_like(edges)
     prepare_steps(offsets, shifts)
-    prepare_sources(region, sources, weights, moments)
+    prepare_sources(region, sources, weights, moments, edge_terms)
     prepare_homes(region, distances, powers, scales, layers)
     terms, nears, strongs = [
         (slots[k : k + BATCH], slots[k + BATCH : k + 2 * BATCH]) for k in range(0, 6 * BATCH, 2 * BATCH)
@@ -315,7 +466,7 @@
 
     def step(index, carry):
         for turn in range(2):
-            first = (2 * index + turn) * BATCH
+            first = (2 * index + turn - 2) * BATCH + EDGE
             for t in range(BATCH):
                 add_forces(
                     pairs, first + t, weights, moments, shifts, nears[turn][t], strongs[turn][t], totals, edges
@@ -324,7 +475,7 @@
                 pair_terms(pairs, first + 2 * BATCH + t, sources, distances, powers, offsets, terms[turn][t])
         return carry
 
-    groups = (count[0] + BATCH - 1) // BATCH
+    groups = -(-(pairs.shape[1] - 2 * EDGE) // BATCH)
     lax.fori_loop(0, (groups + 3) // 2, step, 0)
 
     def finish(block, carry):
@@ -346,12 +497,12 @@
         totals[block] = force + pltpu.roll(force, 4, 0)
         return carry
 
-    lax.fori_loop(0, blocks, finish, 0, unroll=4)
+    lax.fori_loop(0, blocks, finish, 0, unroll=16)
     for axis in range(3):
         out[axis] = totals[:blocks, axis, :]
 
 
-def brick_forces(region, pairs, count, blocks):
+def brick_forces(region, pairs, blocks):
     lines, _, width = region.shape
     single = pltpu.VMEM((blocks + 1, ROWS, width), jnp.float32)
     table = pltpu.VMEM((27, ROWS, width), jnp.float32)
@@ -359,7 +510,6 @@
         force_kernel,
         out_shape=jax.ShapeDtypeStruct((3, blocks, width), jnp.float32),
         in_specs=[
-            pl.BlockSpec(memory_space=pltpu.SMEM),
             pl.BlockSpec(memory_space=pltpu.SMEM),
             pl.BlockSpec(memory_space=pltpu.VMEM),
         ],
@@ -373,12 +523,14 @@
             pltpu.VMEM((blocks + 1, 4 * ROWS, width), jnp.bfloat16),
             single,
             pltpu.VMEM((blocks + 1, ROWS, 4 * ROWS), jnp.float32),
+            pltpu.VMEM((lines, 4 * ROWS, width), jnp.bfloat16),
             table,
             table,
         ]
         + [pltpu.VMEM((width, 2 * width), jnp.float32)] * (2 * BATCH)
         + [pltpu.VMEM((2 * width, width), jnp.bfloat16)] * (4 * BATCH),
-    )(pairs, count, region)
+        compiler_params=pltpu.CompilerParams(vmem_limit_bytes=40 << 20),
+    )(pairs, region)
 
 
 def per_device(coords, charges, atom_types, lj_sigma, lj_epsilon, tile_list):
@@ -386,48 +538,18 @@
     span_z = lax.axis_size("gz")
     blocks = coords.shape[2]
     width = coords.shape[3]
-    layers = blocks // (GRID * GRID)
     ranks = span_y * span_z
-    stride = blocks // ranks
-    dtype = coords.dtype
-    kinds = jnp.arange(lj_sigma.shape[0], dtype=jnp.int32)
-    selector = (atom_types[0][:, :, None] == kinds).astype(dtype)
-    sigma_atom = jnp.sum(selector * (lj_sigma * sigma_scale), axis=2)
-    root_atom = jnp.sum(selector * (jnp.sqrt(lj_epsilon)), axis=2)
-    inner = coords[:, 0] - 0.5 * cell_edge
-    square = inner[0] * inner[0] + inner[1] * inner[1] + inner[2] * inner[2]
-    atoms = jnp.stack(
-        [inner[0], inner[1], inner[2], jnp.ones_like(square), square]
-        + [sigma_atom, root_atom, charges[0] * charge_scale],
-        axis=1,
-    )
-    outgoing = atoms.reshape(stride, ranks, ROWS, width)
-    padded = exchanged(outgoing, layers)
-    region = padded.reshape(-1, ROWS, width)
-    pairs = jnp.pad(
-        tile_list[0, 0, 0], ((0, 0), (2 * BATCH, 4 * BATCH)), constant_values=-1
-    )
-    dead = pairs[0] < 0
-
-    def place(ids):
-        slot = ids // blocks
-        member = ids % blocks
-        px = member // (GRID * layers) + (slot // 9 - 1) * GRID
-        py = member // layers % GRID + (slot // 3 % 3 - 1) * GRID
-        pz = member % layers + (slot % 3 - 1) * layers
-        return px, py, pz
-
-    own = place(jnp.where(dead, 0, pairs[0]) + 13 * blocks)
-    other = place(jnp.where(dead, 13 * blocks, pairs[1]))
-    x, y, z = other
-    line = ((x + 1) * (GRID + 2) + y + 1) * (layers + 2) + z + 1
-    dx, dy, dz = [b - a + 1 for a, b in zip(own, other)]
-    table = jnp.stack([jnp.where(dead, blocks, pairs[0]), line, (dx * 3 + dy) * 3 + dz])
-    count = jnp.sum((~dead).astype(jnp.int32)).reshape(1)
-    totals = brick_forces(region, table, count, blocks)
-    sending = totals.reshape(3, ranks, stride, width)[:, :, :, None]
-    returned = lax.all_to_all(sending, ("gy", "gz"), split_axis=1, concat_axis=3, tiled=True)
-    return returned.reshape(3, 1, blocks, width)
+    padded, table = exchanged(
+        coords[:, 0],
+        charges[0],
+        atom_types[0],
+        lj_sigma[None],
+        lj_epsilon[None],
+        tile_list[0, 0, 0],
+        ranks,
+    )
+    forces = brick_forces(padded.reshape(-1, ROWS, width), table, blocks)
+    return returned(forces, ranks)
 
 
 def solution(mesh):

time: 113 us -> 79.9 us (0.71)
  blocking collectives: 13.1 us -> 0 us
  Pallas kernels: 87 us -> 74.3 us
  other arithmetic: 7.69 us -> 0 us
  local copies, waits for them, and re-layouts: 3.87 us -> 5.28 us
    all_to_all x1 -> x0, blocking collectives: 13.1 us -> none  [per_device(): lax.all_to_all(sending, ('gy', 'gz'), split_axis=1, concat_axis=3, tiled=...]
    pallas_call x1, Pallas kernels: 53.2 us -> 41.8 us  [brick_forces(): pl.pallas_call(force_kernel, out_shape=jax.ShapeDtypeStruct((3, blocks, w...]
    unnamed x2 -> x13, local copies, waits for them, and re-layouts: 0.01 us -> 5.28 us
    reduce_sum x2 -> x0, other arithmetic: 3.66 us -> none  [the longest x1 2.89 us: per_device(): root_atom = jnp.sum(selector * jnp.sqrt(lj_epsilon), axis=2)]
    another operation x3 -> x0, local copies, waits for them, and re-layouts: 2.45 us -> none  [the longest x2 1.51 us: per_device(): jnp.stack([inner[0], inner[1], inner[2], jnp.ones_like(square), square] +...]
    mul x2 -> x0, other arithmetic: 1.51 us -> none  [the longest x1 0.85 us: per_device(): charges[0] * charge_scale]
    pallas_call x1 -> x2, Pallas kernels: 33.8 us -> 32.5 us  [the longest x1 27.1 us: exchanged(): pl.pallas_call(exchange_kernel, out_shape=(jax.ShapeDtypeStruct((GRID + 2...]
where the time goes in v1:
time: 79.9 us; the launch traced here: 79.6 us
  Pallas kernels  74.3 us (93%)
  local copies, waits for them, and re-layouts  5.28 us (7%)
    pallas_call x1, Pallas kernels, brick_forces(): pl.pallas_call(force_kernel, out_shape=jax.ShapeDtypeStruct((3, blocks, w...  41.8 us
    pallas_call x1, Pallas kernels, exchanged(): pl.pallas_call(exchange_kernel, out_shape=(jax.ShapeDtypeStruct((GRID + 2...  27.1 us
    pallas_call x1, Pallas kernels, returned(): pl.pallas_call(return_kernel, out_shape=jax.ShapeDtypeStruct((axes, strid...  5.44 us
    unnamed x13, local copies, waits for them, and re-layouts  5.28 us

profile of v1, /device:TPU:0, one launch (start us, length us, event | category | flops | bytes accessed | tf_op | source)
XLA Modules:
  0.0 79.6 jit_solution(11866810582571466893)
XLA Ops:
  0.0 0.0 copy-start
  0.0 0.9 %copy-done = f32[3,1,128,128]{3,2,1,0:T(8,128)S(1)} copy-done((f32[3,1,128,128]{3,2,1,0:T(8,128)S(1)}, f32[3,1,128,128]{3,2,1,0:T(8,128)}, u32[]{:S(2)}) %copy-start) | copy-done | bytes 196632
  0.9 0.0 copy-start.1
  0.9 0.8 %copy-done.1 = f32[1,128,128]{2,1,0:T(8,128)S(1)} copy-done((f32[1,128,128]{2,1,0:T(8,128)S(1)}, f32[1,128,128]{2,1,0:T(8,128)}, u32[]{:S(2)}) %copy-start.1) | copy-done | bytes 65560
  1.8 0.0 copy-start.2
  1.8 0.8 %copy-done.2 = s32[1,128,128]{2,1,0:T(8,128)S(1)} copy-done((s32[1,128,128]{2,1,0:T(8,128)S(1)}, s32[1,128,128]{2,1,0:T(8,128)}, u32[]{:S(2)}) %copy-start.2) | copy-done | bytes 65560
  2.6 0.0 copy-start.3
  2.6 0.7 copy-done.3
  3.3 0.0 copy-start.4
  3.3 0.7 copy-done.4
  4.0 0.0 copy-start.5
  4.0 0.7 copy-done.5
  4.6 27.1 %shard_map.64 = (f32[6,6,10,8,128]{4,3,2,1,0:T(8,128)S(1)}, s32[8,768]{1,0:T(8,128)S(1)}) custom-call(f32[3,128,128]{2,1,0:T(8,128)S(1)} %bitcast.14, f32[128,128]{1,0:T(8,128)S(1)} %bitcast.15, s32[128,128]{1,0:T(8,128)S(1)} %bitcast.16, f32[1,64]{1,0:T(1,128)S(1)} %bitcast.18, f32[1,64]{1,0:T(1,128)S(1)} %bitcast.19, s32[2,512]{1,0:T(2,128)S(1)} %bitcast.17), custom_call_target="tpu_custom_call" | custom-call | tf_op jit(solution)/shard_map/pallas_call | solution.py:183
  31.7 41.8 %shard_map.65 = f32[3,128,128]{2,1,0:T(8,128)S(1)} custom-call(s32[8,768]{1,0:T(8,128)S(1)} %get-tuple-element.7.pairs, f32[360,8,128]{2,1,0:T(8,128)S(1)} %bitcast.11), custom_call_target="tpu_custom_call" | custom-call | tf_op jit(solution)/shard_map/pallas_call | solution.py:509
  73.5 5.4 %shard_map.66 = f32[3,16,8,1,128]{4,3,2,1,0:T(1,128)S(1)} custom-call(f32[3,8,16,1,128]{4,3,2,1,0:T(1,128)S(1)} %bitcast.12), custom_call_target="tpu_custom_call" | custom-call | tf_op jit(solution)/shard_map/pallas_call | solution.py:235
  78.9 0.7 copy.9
Async XLA Ops:
  0.0 0.9 %copy-start = (f32[3,1,128,128]{3,2,1,0:T(8,128)S(1)}, f32[3,1,128,128]{3,2,1,0:T(8,128)}, u32[]{:S(2)}) copy-start(f32[3,1,128,128]{3,2,1,0:T(8,128)} %param.6) | copy-start | bytes 589828
  0.9 0.8 %copy-start.1 = (f32[1,128,128]{2,1,0:T(8,128)S(1)}, f32[1,128,128]{2,1,0:T(8,128)}, u32[]{:S(2)}) copy-start(f32[1,128,128]{2,1,0:T(8,128)} %param.7) | copy-start | bytes 196612
  1.8 0.8 %copy-start.2 = (s32[1,128,128]{2,1,0:T(8,128)S(1)}, s32[1,128,128]{2,1,0:T(8,128)}, u32[]{:S(2)}) copy-start(s32[1,128,128]{2,1,0:T(8,128)} %param.8) | copy-start | bytes 196612
  2.6 0.7 copy-start.3
  3.3 0.7 copy-start.4
  4.0 0.7 copy-start.5

commit v2 on v1

--- a/solution.py
+++ b/solution.py
@@ -10,7 +10,8 @@
 
 GRID = 4
 ROWS = 8
-BATCH = 4
+BATCH = 8
+HALF = BATCH // 2
 EDGE = 128
 
 cell_edge = 11.0
@@ -49,23 +50,23 @@
 
 
 def looked_up(values, kinds):
-    padded = jnp.concatenate([values, jnp.zeros((1, kinds.shape[1] - values.shape[1]), values.dtype)], axis=1)
-    return jnp.take_along_axis(jnp.broadcast_to(padded, kinds.shape), kinds, axis=1)
-
-
-def pack_atoms(coords, charges, kinds, sigma, epsilon, atoms):
+    return jnp.take_along_axis(jnp.broadcast_to(values, kinds.shape), kinds, axis=1)
+
+
+def pack_atoms(coords, charges, kinds, atoms, labels):
     stride, ranks = atoms.shape[:2]
-    sigmas = sigma[...] * sigma_scale
-    roots = jnp.sqrt(epsilon[...])
     for group in range(stride):
         rows = pl.ds(group * ranks, ranks)
-        inner = [coords[axis, rows, :] - 0.5 * cell_edge for axis in range(3)]
-        kind = kinds[rows, :]
-        square = inner[0] * inner[0] + inner[1] * inner[1] + inner[2] * inner[2]
-        values = inner + [jnp.ones_like(square), square, looked_up(sigmas, kind), looked_up(roots, kind)]
-        values.append(charges[rows, :] * charge_scale)
-        for row, value in enumerate(values):
-            atoms[group, :, row, :] = value
+        for axis in range(3):
+            atoms[group, :, axis, :] = coords[axis, rows, :] - 0.5 * cell_edge
+        atoms[group, :, 3, :] = charges[rows, :] * charge_scale
+        labels[group, :, 0, :] = kinds[rows, :].astype(jnp.float32)
+
+
+def type_table(sigma, epsilon, types):
+    empty = jnp.zeros((1, types.shape[1] - sigma.shape[1]), types.dtype)
+    types[0:1, :] = jnp.concatenate([sigma[...] * sigma_scale, empty], axis=1)
+    types[1:2, :] = jnp.concatenate([jnp.sqrt(epsilon[...]), empty], axis=1)
 
 
 def cell_of(member, layers):
@@ -101,54 +102,64 @@
     table[2:3, EDGE : EDGE + width] = (delta[0] * 3 + delta[1]) * 3 + delta[2]
 
 
-def exchange_kernel(
-    coords, charges, kinds, sigma, epsilon, tiles, region, table, atoms, send_own, recv_own, send_rim, recv_rim, own_sem
-):
+def exchange_kernel(*refs):
+    given, (region, marks, table, types), scratch = refs[:6], refs[6:10], refs[10:]
+    held, (atoms, labels, send_own, recv_own, send_rim, recv_rim, own_sem, load_sem) = scratch[:6], scratch[6:]
     stride, ranks = atoms.shape[:2]
     layers = region.shape[2] - 2
     blocks = stride * ranks
     spans, here = spans_of()
     me = here[1] * spans[2] + here[2]
+    loads = [pltpu.make_async_copy(src, dst, load_sem.at[k]) for k, (src, dst) in enumerate(zip(given, held))]
+    for load in loads:
+        load.start()
     peers = list(plane_peers(spans, here))
     neighbours = list(brick_neighbours(spans, here))
     barrier, greeted = greet([p[2] for p in peers] + [n[1] for n in neighbours])
-    pack_atoms(coords, charges, kinds, sigma, epsilon, atoms)
+    coords, charges, kinds, sigma, epsilon, tiles = held
+    for load in loads:
+        load.wait()
+    pack_atoms(coords, charges, kinds, atoms, labels)
     tile_table(tiles, table, blocks, layers)
+    type_table(sigma, epsilon, types)
     pl.semaphore_wait(barrier, greeted)
     chunk = math.gcd(stride, layers)
     pieces = stride // chunk
-
-    def place(piece):
+    pairs = ((atoms, region), (labels, marks))
+
+    def place(ref, piece):
         x, y, z = cell_of(me * stride + piece * chunk, layers)
-        return region.at[x + 1, y + 1, pl.ds(z + 1, chunk)]
+        return ref.at[x + 1, y + 1, pl.ds(z + 1, chunk)]
 
     copies = []
     for hop, to, device in peers:
         for piece in range(pieces):
-            sem = (hop - 1) * pieces + piece
-            copies.append(
-                pltpu.make_async_remote_copy(
-                    src_ref=atoms.at[pl.ds(piece * chunk, chunk), to],
-                    dst_ref=place(piece),
-                    send_sem=send_own.at[sem],
-                    recv_sem=recv_own.at[sem],
-                    device_id=device,
-                    device_id_type=pl.DeviceIdType.MESH,
+            for k, (source, target) in enumerate(pairs):
+                sem = ((hop - 1) * pieces + piece) * 2 + k
+                copies.append(
+                    pltpu.make_async_remote_copy(
+                        src_ref=source.at[pl.ds(piece * chunk, chunk), to],
+                        dst_ref=place(target, piece),
+                        send_sem=send_own.at[sem],
+                        recv_sem=recv_own.at[sem],
+                        device_id=device,
+                        device_id_type=pl.DeviceIdType.MESH,
+                    )
                 )
+                copies[-1].start()
+    for piece in range(pieces):
+        for k, (source, target) in enumerate(pairs):
+            kept = pltpu.make_async_copy(
+                source.at[pl.ds(piece * chunk, chunk), me], place(target, piece), own_sem.at[piece * 2 + k]
             )
-            copies[-1].start()
-    for piece in range(pieces):
-        kept = pltpu.make_async_copy(
-            atoms.at[pl.ds(piece * chunk, chunk), me], place(piece), own_sem.at[piece]
-        )
-        kept.start()
-        copies.append(kept)
+            kept.start()
+            copies.append(kept)
     for copy in copies:
         copy.wait()
 
     lengths = (GRID, GRID, layers)
     rims = []
-    for sem, (offset, device) in enumerate(neighbours):
+    for index, (offset, device) in enumerate(neighbours):
         source = tuple(
             pl.ds(1, n) if o == 0 else pl.ds(n if o > 0 else 1, 1)
             for o, n in zip(offset, lengths)
@@ -157,49 +168,57 @@
             pl.ds(1, n) if o == 0 else pl.ds(0 if o > 0 else n + 1, 1)
             for o, n in zip(offset, lengths)
         )
-        rims.append(
-            pltpu.make_async_remote_copy(
-                src_ref=region.at[source],
-                dst_ref=region.at[target],
-                send_sem=send_rim.at[sem],
-                recv_sem=recv_rim.at[sem],
-                device_id=device,
-                device_id_type=pl.DeviceIdType.MESH,
+        for k, ref in enumerate((region, marks)):
+            rims.append(
+                pltpu.make_async_remote_copy(
+                    src_ref=ref.at[source],
+                    dst_ref=ref.at[target],
+                    send_sem=send_rim.at[index * 2 + k],
+                    recv_sem=recv_rim.at[index * 2 + k],
+                    device_id=device,
+                    device_id_type=pl.DeviceIdType.MESH,
+                )
             )
-        )
-        rims[-1].start()
+            rims[-1].start()
     for copy in rims:
         copy.wait()
 
 
-def exchanged(coords, charges, kinds, sigma, epsilon, tiles, ranks):
+def exchanged(given, ranks):
+    coords, charges, _, _, _, tiles = given
     blocks, width = charges.shape
     layers = blocks // (GRID * GRID)
     stride = blocks // ranks
     pieces = stride // math.gcd(stride, layers)
-    own = pltpu.SemaphoreType.DMA(((ranks - 1) * pieces,))
-    rim = pltpu.SemaphoreType.DMA((26,))
+    own = pltpu.SemaphoreType.DMA(((ranks - 1) * pieces * 2,))
+    rim = pltpu.SemaphoreType.DMA((52,))
     vmem = pl.BlockSpec(memory_space=pltpu.VMEM)
+    cells = (GRID + 2, GRID + 2, layers + 2)
     return pl.pallas_call(
         exchange_kernel,
         out_shape=(
-            jax.ShapeDtypeStruct((GRID + 2, GRID + 2, layers + 2, ROWS, width), coords.dtype),
+            jax.ShapeDtypeStruct((*cells, 4, width), coords.dtype),
+            jax.ShapeDtypeStruct((*cells, 1, width), coords.dtype),
             jax.ShapeDtypeStruct((ROWS, tiles.shape[1] + 2 * EDGE), jnp.int32),
+            jax.ShapeDtypeStruct((ROWS, width), coords.dtype),
         ),
-        in_specs=[vmem] * 6,
-        out_specs=(vmem, vmem),
-        scratch_shapes=[
-            pltpu.VMEM((stride, ranks, ROWS, width), coords.dtype),
+        in_specs=[pl.BlockSpec(memory_space=pltpu.HBM)] * 6,
+        out_specs=(vmem,) * 4,
+        scratch_shapes=[pltpu.VMEM(x.shape, x.dtype) for x in given]
+        + [
+            pltpu.VMEM((stride, ranks, 4, width), coords.dtype),
+            pltpu.VMEM((stride, ranks, 1, width), coords.dtype),
             own,
             own,
             rim,
             rim,
-            pltpu.SemaphoreType.DMA((pieces,)),
+            pltpu.SemaphoreType.DMA((pieces * 2,)),
+            pltpu.SemaphoreType.DMA((6,)),
         ],
         compiler_params=pltpu.CompilerParams(
             has_side_effects=True, collective_id=0, vmem_limit_bytes=8 << 20
         ),
-    )(coords, charges, kinds, sigma, epsilon, tiles)
+    )(*given)
 
 
 def return_kernel(forces, out, send, recv, own_sem):
@@ -289,8 +308,33 @@
     return out * jnp.where(rows // 4 % 2 == 1, four, 1.0)
 
 
-def prepare_sources(region, sources, weights, moments, edge_terms):
-    shape = region.shape[1:]
+def prepare_types(marks, types, sigmas, roots):
+    def one(group, carry):
+        rows = pl.ds(pl.multiple_of(group * ROWS, ROWS), ROWS)
+        kind = marks[rows, :].astype(jnp.int32)
+        sigmas[rows, :] = looked_up(types[0:1, :], kind)
+        roots[rows, :] = looked_up(types[1:2, :], kind)
+        return carry
+
+    lax.fori_loop(0, marks.shape[0] // ROWS, one, 0, unroll=5)
+
+
+def spread_row(ref, line, shape):
+    return jnp.broadcast_to(ref[pl.ds(line, 1), :], shape)
+
+
+def places(region, line):
+    block = jnp.concatenate([region[line], region[line]], axis=0)
+    return jnp.where(rows_of(block.shape) % 4 == 3, 1.0, block)
+
+
+def scaled(region, roots, line, shape):
+    charge = jnp.broadcast_to(region[line, 3:4, :], shape)
+    return jnp.where(rows_of(shape) < 4, spread_row(roots, line, shape), charge)
+
+
+def prepare_sources(region, sigmas, roots, sources, weights, moments, edge_terms):
+    shape = (ROWS, region.shape[2])
     rows = rows_of(shape)
     count = moments.shape[2]
     ways = row_table([math.comb(6, k) for k in range(7)], shape)
@@ -303,17 +347,14 @@
     kept = (rows_of((ROWS, count)) >= 4) == (lanes % (2 * ROWS) == 7)
 
     def spread(line):
-        block = region[line]
-        high, middle, low = split(block)
-        sigma = jnp.broadcast_to(region[line, 5:6, :], shape)
-        root = jnp.broadcast_to(region[line, 6:7, :], shape)
-        charge = jnp.broadcast_to(region[line, 7:8, :], shape)
+        place = places(region, line)
+        high, middle, low = split(place * jnp.where(rows < 4, 1.0, place))
+        sigma = spread_row(sigmas, line, shape)
         falling = rising_powers(sigma, 6 - jnp.minimum(rows, 6))
         square = sigma * sigma
         top, rest, _ = split(ways * falling)
         sources[line] = stacked([high, middle, high, middle, high, low, top, rest, top, rest])
-        place = jnp.where(rows < 4, block, pltpu.roll(block, 4, 0))
-        top, rest, _ = split(place * jnp.where(rows < 4, root, charge))
+        top, rest, _ = split(place * scaled(region, roots, line, shape))
         weights[line] = stacked([top, rest])
         first = split(falling * (high_at * (square * square * square) + low_at) + near_at)
         second = split(falling * wide_at)
@@ -345,20 +386,18 @@
         summed(lines - group + k)
 
 
-def prepare_homes(region, distances, powers, scales, layers):
-    shape = region.shape[1:]
+def prepare_homes(region, sigmas, roots, distances, powers, scales, layers):
+    shape = distances.shape[1:]
     rows = rows_of(shape)
     blocks = distances.shape[0] - 1
 
     def one(block, carry):
         line = own_line(block, layers)
-        home = region[line]
-        distances[block] = jnp.where(rows < 3, -2.0 * home, jnp.where(rows == 4, 1.0, 0.0))
-        top, rest, _ = split(rising_powers(jnp.broadcast_to(region[line, 5:6, :], shape), rows))
+        home = places(region, line)
+        distances[block] = jnp.where(rows < 3, -2.0 * home, jnp.where(rows % 4 < 3, 1.0, 0.0))
+        top, rest, _ = split(rising_powers(spread_row(sigmas, line, shape), rows))
         powers[block] = stacked([top, top, rest, rest])
-        root = jnp.broadcast_to(region[line, 6:7, :], shape)
-        charge = jnp.broadcast_to(region[line, 7:8, :], shape)
-        scales[block] = 12.0 * jnp.where(rows < 4, root, charge)
+        scales[block] = 12.0 * scaled(region, roots, line, shape)
         return carry
 
     lax.fori_loop(0, blocks, one, 0, unroll=4)
@@ -451,38 +490,51 @@
 
 
 def force_kernel(
-    pairs, region, out, totals, sources, weights, moments, distances, powers, scales, edges, edge_terms, offsets, shifts, *slots
+    pairs, region, marks, types, out, totals, sources, weights, moments, distances, powers, scales, edges, edge_terms,
+    sigmas, roots, offsets, shifts, *slots
 ):
     blocks = out.shape[1]
     layers = blocks // (GRID * GRID)
     totals[...] = jnp.zeros_like(totals)
     edges[...] = jnp.zeros_like(edges)
+    prepare_types(marks, types, sigmas, roots)
     prepare_steps(offsets, shifts)
-    prepare_sources(region, sources, weights, moments, edge_terms)
-    prepare_homes(region, distances, powers, scales, layers)
-    terms, nears, strongs = [
-        (slots[k : k + BATCH], slots[k + BATCH : k + 2 * BATCH]) for k in range(0, 6 * BATCH, 2 * BATCH)
-    ]
+    prepare_sources(region, sigmas, roots, sources, weights, moments, edge_terms)
+    prepare_homes(region, sigmas, roots, distances, powers, scales, layers)
+    terms, nears, strongs = [slots[k : k + BATCH] for k in range(0, 3 * BATCH, BATCH)]
 
     def step(index, carry):
-        for turn in range(2):
-            first = (2 * index + turn - 2) * BATCH + EDGE
-            for t in range(BATCH):
-                add_forces(
-                    pairs, first + t, weights, moments, shifts, nears[turn][t], strongs[turn][t], totals, edges
-                )
-                strengths(terms[1 - turn][t], nears[1 - turn][t], strongs[1 - turn][t])
-                pair_terms(pairs, first + 2 * BATCH + t, sources, distances, powers, offsets, terms[turn][t])
+        first = (index - 1) * BATCH + EDGE
+
+        def push(t, lag):
+            add_forces(
+                pairs, first - lag + t, weights, moments, shifts, nears[t], strongs[t], totals, edges
+            )
+
+        def pull(t):
+            strengths(terms[t], nears[t], strongs[t])
+
+        def pair(t):
+            pair_terms(pairs, first + BATCH + t, sources, distances, powers, offsets, terms[t])
+
+        for t in range(HALF):
+            pull(t)
+            push(HALF + t, BATCH)
+            pair(t)
+        for t in range(HALF):
+            pull(HALF + t)
+            push(t, 0)
+            pair(HALF + t)
         return carry
 
     groups = -(-(pairs.shape[1] - 2 * EDGE) // BATCH)
-    lax.fori_loop(0, (groups + 3) // 2, step, 0)
+    lax.fori_loop(0, groups + 2, step, 0)
 
     def finish(block, carry):
-        home = region[own_line(block, layers)]
-        rows = rows_of(home.shape)
-        place = jnp.where(rows < 4, home, pltpu.roll(home, 4, 0))
-        sigma = jnp.broadcast_to(home[5:6], home.shape)
+        line = own_line(block, layers)
+        place = places(region, line)
+        rows = rows_of(place.shape)
+        sigma = spread_row(sigmas, line, place.shape)
         rising = rising_powers(sigma, rows)
         square = sigma * sigma
         first = split(jnp.where(rows == 7, 1.0, rising))
@@ -502,7 +554,7 @@
         out[axis] = totals[:blocks, axis, :]
 
 
-def brick_forces(region, pairs, blocks):
+def brick_forces(region, marks, pairs, types, blocks):
     lines, _, width = region.shape
     single = pltpu.VMEM((blocks + 1, ROWS, width), jnp.float32)
     table = pltpu.VMEM((27, ROWS, width), jnp.float32)
@@ -511,6 +563,8 @@
         out_shape=jax.ShapeDtypeStruct((3, blocks, width), jnp.float32),
         in_specs=[
             pl.BlockSpec(memory_space=pltpu.SMEM),
+            pl.BlockSpec(memory_space=pltpu.VMEM),
+            pl.BlockSpec(memory_space=pltpu.VMEM),
             pl.BlockSpec(memory_space=pltpu.VMEM),
         ],
         out_specs=pl.BlockSpec(memory_space=pltpu.VMEM),
@@ -524,13 +578,15 @@
             single,
             pltpu.VMEM((blocks + 1, ROWS, 4 * ROWS), jnp.float32),
             pltpu.VMEM((lines, 4 * ROWS, width), jnp.bfloat16),
+            pltpu.VMEM((lines, width), jnp.float32),
+            pltpu.VMEM((lines, width), jnp.float32),
             table,
             table,
         ]
-        + [pltpu.VMEM((width, 2 * width), jnp.float32)] * (2 * BATCH)
-        + [pltpu.VMEM((2 * width, width), jnp.bfloat16)] * (4 * BATCH),
+        + [pltpu.VMEM((width, 2 * width), jnp.float32)] * BATCH
+        + [pltpu.VMEM((2 * width, width), jnp.bfloat16)] * (2 * BATCH),
         compiler_params=pltpu.CompilerParams(vmem_limit_bytes=40 << 20),
-    )(pairs, region)
+    )(pairs, region, marks, types)
 
 
 def per_device(coords, charges, atom_types, lj_sigma, lj_epsilon, tile_list):
@@ -539,16 +595,11 @@
     blocks = coords.shape[2]
     width = coords.shape[3]
     ranks = span_y * span_z
-    padded, table = exchanged(
-        coords[:, 0],
-        charges[0],
-        atom_types[0],
-        lj_sigma[None],
-        lj_epsilon[None],
-        tile_list[0, 0, 0],
-        ranks,
+    given = (coords[:, 0], charges[0], atom_types[0], lj_sigma[None], lj_epsilon[None], tile_list[0, 0, 0])
+    region, marks, table, types = exchanged(given, ranks)
+    forces = brick_forces(
+        region.reshape(-1, 4, width), marks.reshape(-1, width), table, types, blocks
     )
-    forces = brick_forces(padded.reshape(-1, ROWS, width), table, blocks)
     return returned(forces, ranks)
 
 

time: 79.9 us -> 71.8 us (0.90)
  Pallas kernels: 74.3 us -> 67.5 us
  local copies, waits for them, and re-layouts: 5.28 us -> 3.97 us
    pallas_call x1, Pallas kernels: 27.1 us -> 23.4 us  [exchanged(): pl.pallas_call(exchange_kernel, out_shape=(jax.ShapeDtypeStruct((*cells,...]
    pallas_call x1, Pallas kernels: 41.8 us -> 38.8 us  [brick_forces(): pl.pallas_call(force_kernel, out_shape=jax.ShapeDtypeStruct((3, blocks, w...]
    unnamed x13, local copies, waits for them, and re-layouts: 5.28 us -> 3.97 us
where the time goes in v2:
time: 71.8 us; the launch traced here: 71.5 us
  Pallas kernels  67.5 us (94%)
  local copies, waits for them, and re-layouts  3.97 us (6%)
    pallas_call x1, Pallas kernels, brick_forces(): pl.pallas_call(force_kernel, out_shape=jax.ShapeDtypeStruct((3, blocks, w...  38.8 us
    pallas_call x1, Pallas kernels, exchanged(): pl.pallas_call(exchange_kernel, out_shape=(jax.ShapeDtypeStruct((*cells,...  23.4 us
    pallas_call x1, Pallas kernels, returned(): pl.pallas_call(return_kernel, out_shape=jax.ShapeDtypeStruct((axes, strid...  5.36 us
    unnamed x13, local copies, waits for them, and re-layouts  3.97 us

profile of v2, /device:TPU:0, one launch (start us, length us, event | category | flops | bytes accessed | tf_op | source)
XLA Modules:
  0.0 71.5 jit_solution(5879234419920317368)
XLA Ops:
  0.0 0.0 copy-start.3
  0.0 0.0 copy-start.4
  0.0 0.0 copy-start.5
  0.0 0.7 copy-done.3
  0.7 0.0 copy-done.4
  0.7 0.0 copy-done.5
  0.7 0.0 copy-start
  0.7 0.9 %copy-done = f32[3,1,128,128]{3,2,1,0:T(8,128)S(1)} copy-done((f32[3,1,128,128]{3,2,1,0:T(8,128)S(1)}, f32[3,1,128,128]{3,2,1,0:T(8,128)}, u32[]{:S(2)}) %copy-start) | copy-done | bytes 196632
  1.6 0.0 copy-start.1
  1.6 0.8 %copy-done.1 = f32[1,128,128]{2,1,0:T(8,128)S(1)} copy-done((f32[1,128,128]{2,1,0:T(8,128)S(1)}, f32[1,128,128]{2,1,0:T(8,128)}, u32[]{:S(2)}) %copy-start.1) | copy-done | bytes 65560
  2.5 0.0 copy-start.2
  2.5 0.8 %copy-done.2 = s32[1,128,128]{2,1,0:T(8,128)S(1)} copy-done((s32[1,128,128]{2,1,0:T(8,128)S(1)}, s32[1,128,128]{2,1,0:T(8,128)}, u32[]{:S(2)}) %copy-start.2) | copy-done | bytes 65560
  3.3 23.4 %shard_map.64 = (f32[6,6,10,4,128]{4,3,2,1,0:T(4,128)S(1)}, f32[6,6,10,1,128]{4,3,2,1,0:T(1,128)S(1)}, s32[8,768]{1,0:T(8,128)S(1)}, f32[8,128]{1,0:T(8,128)S(1)}) custom-call(f32[3,128,128]{2,1,0:T(8,128)S(1)} %bitcast.15, f32[128,128]{1,0:T(8,128)S(1)} %bitcast.17, s32[128,128]{1,0:T(8,128)S(1)} %bitcast.18, f32[1,64]{1,0:T(1,128)S(1)} %bitcast.20, ...), custom_call_target="tpu_custom_call" | custom-call | tf_op jit(solution)/shard_map/pallas_call | solution.py:197
  26.7 38.8 %shard_map.65 = f32[3,128,128]{2,1,0:T(8,128)S(1)} custom-call(s32[8,768]{1,0:T(8,128)S(1)} %get-tuple-element.9.pairs, f32[360,4,128]{2,1,0:T(4,128)S(1)} %bitcast.14, f32[360,128]{1,0:T(8,128)S(1)} %bitcast.16, f32[8,128]{1,0:T(8,128)S(1)} %get-tuple-element.12.types), custom_call_target="tpu_custom_call" | custom-call | tf_op jit(solution)/shard_map/pallas_call | solution.py:561
  65.5 5.4 %shard_map.66 = f32[3,16,8,1,128]{4,3,2,1,0:T(1,128)S(1)} custom-call(f32[3,8,16,1,128]{4,3,2,1,0:T(1,128)S(1)} %bitcast.12), custom_call_target="tpu_custom_call" | custom-call | tf_op jit(solution)/shard_map/pallas_call | solution.py:254
  70.9 0.7 copy.9
Async XLA Ops:
  0.0 0.7 copy-start.3
  0.0 0.7 copy-start.4
  0.0 0.7 copy-start.5
  0.7 0.9 %copy-start = (f32[3,1,128,128]{3,2,1,0:T(8,128)S(1)}, f32[3,1,128,128]{3,2,1,0:T(8,128)}, u32[]{:S(2)}) copy-start(f32[3,1,128,128]{3,2,1,0:T(8,128)} %param.6) | copy-start | bytes 589828
  1.6 0.8 %copy-start.1 = (f32[1,128,128]{2,1,0:T(8,128)S(1)}, f32[1,128,128]{2,1,0:T(8,128)}, u32[]{:S(2)}) copy-start(f32[1,128,128]{2,1,0:T(8,128)} %param.7) | copy-start | bytes 196612
  2.5 0.8 %copy-start.2 = (s32[1,128,128]{2,1,0:T(8,128)S(1)}, s32[1,128,128]{2,1,0:T(8,128)}, u32[]{:S(2)}) copy-start(s32[1,128,128]{2,1,0:T(8,128)} %param.8) | copy-start | bytes 196612

commit v3 on v2

--- a/solution.py
+++ b/solution.py
@@ -11,8 +11,10 @@
 GRID = 4
 ROWS = 8
 BATCH = 8
-HALF = BATCH // 2
+LAG = 4
 EDGE = 128
+STEPS = 32
+SHARE = 4096
 
 cell_edge = 11.0
 cutoff = 9.0
@@ -53,14 +55,14 @@
     return jnp.take_along_axis(jnp.broadcast_to(values, kinds.shape), kinds, axis=1)
 
 
-def pack_atoms(coords, charges, kinds, atoms, labels):
+def pack_atoms(raw, atoms, labels):
     stride, ranks = atoms.shape[:2]
     for group in range(stride):
         rows = pl.ds(group * ranks, ranks)
         for axis in range(3):
-            atoms[group, :, axis, :] = coords[axis, rows, :] - 0.5 * cell_edge
-        atoms[group, :, 3, :] = charges[rows, :] * charge_scale
-        labels[group, :, 0, :] = kinds[rows, :].astype(jnp.float32)
+            atoms[group, :, axis, :] = raw[axis, rows, :] - 0.5 * cell_edge
+        atoms[group, :, 3, :] = raw[3, rows, :] * charge_scale
+        labels[group, :, 0, :] = raw[4, rows, :]
 
 
 def type_table(sigma, epsilon, types):
@@ -96,15 +98,14 @@
     line = ((there[0] + 1) * (GRID + 2) + there[1] + 1) * (layers + 2) + there[2] + 1
     delta = [t - o + 1 for t, o in zip(there, own)]
     width = tiles.shape[1]
-    table[...] = jnp.where(rows_of(table.shape) == 0, blocks, 0)
-    table[0:1, EDGE : EDGE + width] = jnp.where(dead, blocks, home)
-    table[1:2, EDGE : EDGE + width] = line
-    table[2:3, EDGE : EDGE + width] = (delta[0] * 3 + delta[1]) * 3 + delta[2]
+    step = (delta[0] * 3 + delta[1]) * 3 + delta[2]
+    table[...] = jnp.full(table.shape, blocks * STEPS, jnp.int32)
+    table[:, EDGE : EDGE + width] = (line * SHARE + jnp.where(dead, blocks, home)) * STEPS + step
 
 
 def exchange_kernel(*refs):
-    given, (region, marks, table, types), scratch = refs[:6], refs[6:10], refs[10:]
-    held, (atoms, labels, send_own, recv_own, send_rim, recv_rim, own_sem, load_sem) = scratch[:6], scratch[6:]
+    given, (region, marks, table, types), scratch = refs[:4], refs[4:8], refs[8:]
+    held, (atoms, labels, send_own, recv_own, send_rim, recv_rim, own_sem, load_sem) = scratch[:4], scratch[4:]
     stride, ranks = atoms.shape[:2]
     layers = region.shape[2] - 2
     blocks = stride * ranks
@@ -116,10 +117,10 @@
     peers = list(plane_peers(spans, here))
     neighbours = list(brick_neighbours(spans, here))
     barrier, greeted = greet([p[2] for p in peers] + [n[1] for n in neighbours])
-    coords, charges, kinds, sigma, epsilon, tiles = held
+    raw, sigma, epsilon, tiles = held
     for load in loads:
         load.wait()
-    pack_atoms(coords, charges, kinds, atoms, labels)
+    pack_atoms(raw, atoms, labels)
     tile_table(tiles, table, blocks, layers)
     type_table(sigma, epsilon, types)
     pl.semaphore_wait(barrier, greeted)
@@ -185,8 +186,8 @@
 
 
 def exchanged(given, ranks):
-    coords, charges, _, _, _, tiles = given
-    blocks, width = charges.shape
+    raw, _, _, tiles = given
+    blocks, width = raw.shape[1:]
     layers = blocks // (GRID * GRID)
     stride = blocks // ranks
     pieces = stride // math.gcd(stride, layers)
@@ -197,23 +198,23 @@
     return pl.pallas_call(
         exchange_kernel,
         out_shape=(
-            jax.ShapeDtypeStruct((*cells, 4, width), coords.dtype),
-            jax.ShapeDtypeStruct((*cells, 1, width), coords.dtype),
-            jax.ShapeDtypeStruct((ROWS, tiles.shape[1] + 2 * EDGE), jnp.int32),
-            jax.ShapeDtypeStruct((ROWS, width), coords.dtype),
+            jax.ShapeDtypeStruct((*cells, 4, width), raw.dtype),
+            jax.ShapeDtypeStruct((*cells, 1, width), raw.dtype),
+            jax.ShapeDtypeStruct((1, tiles.shape[1] + 2 * EDGE), jnp.int32),
+            jax.ShapeDtypeStruct((ROWS, width), raw.dtype),
         ),
-        in_specs=[pl.BlockSpec(memory_space=pltpu.HBM)] * 6,
+        in_specs=[pl.BlockSpec(memory_space=pltpu.HBM)] * 4,
         out_specs=(vmem,) * 4,
         scratch_shapes=[pltpu.VMEM(x.shape, x.dtype) for x in given]
         + [
-            pltpu.VMEM((stride, ranks, 4, width), coords.dtype),
-            pltpu.VMEM((stride, ranks, 1, width), coords.dtype),
+            pltpu.VMEM((stride, ranks, 4, width), raw.dtype),
+            pltpu.VMEM((stride, ranks, 1, width), raw.dtype),
             own,
             own,
             rim,
             rim,
             pltpu.SemaphoreType.DMA((pieces * 2,)),
-            pltpu.SemaphoreType.DMA((6,)),
+            pltpu.SemaphoreType.DMA((4,)),
         ],
         compiler_params=pltpu.CompilerParams(
             has_side_effects=True, collective_id=0, vmem_limit_bytes=8 << 20
@@ -316,7 +317,7 @@
         roots[rows, :] = looked_up(types[1:2, :], kind)
         return carry
 
-    lax.fori_loop(0, marks.shape[0] // ROWS, one, 0, unroll=5)
+    lax.fori_loop(0, marks.shape[0] // ROWS, one, 0, unroll=15)
 
 
 def spread_row(ref, line, shape):
@@ -370,7 +371,7 @@
         moments[line] = jnp.where(kept, both[:ROWS] + both[ROWS:], 0.0)
 
     lines = region.shape[0]
-    group = max(n for n in range(1, 25) if lines % n == 0)
+    group = max(n for n in range(1, 41) if lines % n == 0)
 
     def one(index, carry):
         for k in range(group):
@@ -400,7 +401,7 @@
         scales[block] = 12.0 * scaled(region, roots, line, shape)
         return carry
 
-    lax.fori_loop(0, blocks, one, 0, unroll=4)
+    lax.fori_loop(0, blocks, one, 0, unroll=16)
     distances[blocks] = jnp.zeros(shape, jnp.float32)
     powers[blocks] = jnp.zeros(powers.shape[1:], powers.dtype)
 
@@ -419,9 +420,14 @@
         shifts[step] = row_table(moves + [0.0] + moves, shape)
 
 
+def unpacked(pairs, index):
+    entry = pairs[index]
+    return remainder(quotient(entry, STEPS), SHARE), quotient(entry, STEPS * SHARE), remainder(entry, STEPS)
+
+
 def pair_terms(pairs, index, sources, distances, powers, offsets, terms):
-    home = pairs[0, index]
-    distance = distances[home] + offsets[pairs[2, index]]
+    home, line, step = unpacked(pairs, index)
+    distance = distances[home] + offsets[step]
     rows = rows_of(distance.shape)
     share = jnp.where(rows < 3, 0.25, jnp.where(rows == 4, soft_core, 0.0))
     square = jnp.sum(distance * distance * share, axis=0, keepdims=True)
@@ -438,7 +444,7 @@
         axis=1,
     )
     terms[...] = lax.dot_general(
-        sources[pairs[1, index]],
+        sources[line],
         right,
         (((0,), (0,)), ((), ())),
         preferred_element_type=jnp.float32,
@@ -464,7 +470,7 @@
 
 
 def add_forces(pairs, index, weights, moments, shifts, nears, strongs, totals, edges):
-    line = pairs[1, index]
+    home, line, step = unpacked(pairs, index)
     left = weights[line]
     both = jnp.dot(
         jnp.concatenate([left, left], axis=1),
@@ -476,8 +482,7 @@
     rows = rows_of((ROWS, width))
     summed = jnp.where(rows < 4, both[:, width:], both[:, :width])
     plain = jnp.where(rows < 4, summed[3:4], summed[7:8])
-    shift = shifts[pairs[2, index]]
-    home = pairs[0, index]
+    shift = shifts[step]
     totals[home] += summed + shift * plain
     shape = moments.shape[1:]
     count = shape[1]
@@ -517,17 +522,13 @@
         def pair(t):
             pair_terms(pairs, first + BATCH + t, sources, distances, powers, offsets, terms[t])
 
-        for t in range(HALF):
+        for t in range(BATCH):
             pull(t)
-            push(HALF + t, BATCH)
+            push((t - LAG) % BATCH, BATCH if t < LAG else 0)
             pair(t)
-        for t in range(HALF):
-            pull(HALF + t)
-            push(t, 0)
-            pair(HALF + t)
         return carry
 
-    groups = -(-(pairs.shape[1] - 2 * EDGE) // BATCH)
+    groups = -(-(pairs.shape[0] - 2 * EDGE) // BATCH)
     lax.fori_loop(0, groups + 2, step, 0)
 
     def finish(block, carry):
@@ -549,7 +550,7 @@
         totals[block] = force + pltpu.roll(force, 4, 0)
         return carry
 
-    lax.fori_loop(0, blocks, finish, 0, unroll=16)
+    lax.fori_loop(0, blocks, finish, 0, unroll=64)
     for axis in range(3):
         out[axis] = totals[:blocks, axis, :]
 
@@ -595,10 +596,11 @@
     blocks = coords.shape[2]
     width = coords.shape[3]
     ranks = span_y * span_z
-    given = (coords[:, 0], charges[0], atom_types[0], lj_sigma[None], lj_epsilon[None], tile_list[0, 0, 0])
+    raw = jnp.concatenate([coords[:, 0], charges, atom_types.astype(coords.dtype)], axis=0)
+    given = (raw, lj_sigma[None], lj_epsilon[None], tile_list[0, 0, 0])
     region, marks, table, types = exchanged(given, ranks)
     forces = brick_forces(
-        region.reshape(-1, 4, width), marks.reshape(-1, width), table, types, blocks
+        region.reshape(-1, 4, width), marks.reshape(-1, width), table.reshape(-1), types, blocks
     )
     return returned(forces, ranks)
 

time: 71.8 us -> 68.1 us (0.948)
  local copies, waits for them, and re-layouts: 3.97 us -> 0.7 us
  Pallas kernels: 67.5 us -> 65.3 us
  other arithmetic: 0 us -> 1.86 us
    unnamed x13 -> x9, local copies, waits for them, and re-layouts: 3.97 us -> 0.7 us
    pallas_call x1, Pallas kernels: 38.8 us -> 36.7 us  [brick_forces(): pl.pallas_call(force_kernel, out_shape=jax.ShapeDtypeStruct((3, blocks, w...]
    concatenate x0 -> x1, other arithmetic: none -> 0.97 us  [per_device(): jnp.concatenate([coords[:, 0], charges, atom_types.astype(coords.dtype)],...]
    convert_element_type x0 -> x1, other arithmetic: none -> 0.88 us  [per_device(): atom_types.astype(coords.dtype)]
where the time goes in v3:
time: 68.1 us; the launch traced here: 67.9 us
  Pallas kernels  65.3 us (96%)
  other arithmetic  1.86 us (3%)
  local copies, waits for them, and re-layouts  0.7 us (1%)
    pallas_call x1, Pallas kernels, brick_forces(): pl.pallas_call(force_kernel, out_shape=jax.ShapeDtypeStruct((3, blocks, w...  36.7 us
    pallas_call x1, Pallas kernels, exchanged(): pl.pallas_call(exchange_kernel, out_shape=(jax.ShapeDtypeStruct((*cells,...  23.1 us
    pallas_call x1, Pallas kernels, returned(): pl.pallas_call(return_kernel, out_shape=jax.ShapeDtypeStruct((axes, strid...  5.4 us

profile of v3, /device:TPU:0, one launch (start us, length us, event | category | flops | bytes accessed | tf_op | source)
XLA Modules:
  0.0 67.9 jit_solution(8604175607239663410)
XLA Ops:
  0.0 0.0 copy-start.3
  0.0 0.9 %convert_element_type.3 = f32[1,128,128]{2,1,0:T(8,128)S(1)} convert(s32[1,128,128]{2,1,0:T(8,128)} %param.8) | non-fusion elementwise | flops 16384 | bytes 131072 | tf_op jit(solution)/shard_map/convert_element_type | solution.py:599
  0.9 0.0 copy-done.3
  0.9 0.0 copy-start
  0.9 0.0 copy-start.1
  0.9 0.0 copy-start.2
  0.9 1.0 %pad_maximum_fusion.refs_0_ = f32[5,128,128]{2,1,0:T(8,128)S(1)} fusion(f32[1,128,128]{2,1,0:T(8,128)S(1)} %convert_element_type.3, f32[1,128,128]{2,1,0:T(8,128)S(1)} %copy-done.3, f32[3,128,128]{2,1,0:T(8,128)} %bitcast.17), kind=kLoop, calls=%fused_computation | loop fusion | flops 163840 | bytes 655360 | tf_op jit(solution)/shard_map/concatenate | solution.py:599
  1.9 0.0 copy-done
  1.9 0.0 copy-done.1
  1.9 0.0 copy-done.2
  1.9 23.1 %shard_map.64 = (f32[6,6,10,4,128]{4,3,2,1,0:T(4,128)S(1)}, f32[6,6,10,1,128]{4,3,2,1,0:T(1,128)S(1)}, s32[1,768]{1,0:T(1,128)S(1)}, f32[8,128]{1,0:T(8,128)S(1)}) custom-call(f32[5,128,128]{2,1,0:T(8,128)S(1)} %pad_maximum_fusion.refs_0_, f32[1,64]{1,0:T(1,128)S(1)} %bitcast.15, f32[1,64]{1,0:T(1,128)S(1)} %bitcast.16, s32[2,512]{1,0:T(2,128)S(1)} %bitcast.14), custom_call_target="tpu_custom_call" | custom-call | tf_op jit(solution)/shard_map/pallas_call | solution.py:198
  25.1 36.7 %shard_map.65 = f32[3,128,128]{2,1,0:T(8,128)S(1)} custom-call(s32[768]{0:T(1024)S(1)} %reduce.pairs, f32[360,4,128]{2,1,0:T(4,128)S(1)} %bitcast.12, f32[360,128]{1,0:T(8,128)S(1)} %bitcast.13, f32[8,128]{1,0:T(8,128)S(1)} %get-tuple-element.12.types), custom_call_target="tpu_custom_call" | custom-call | tf_op jit(solution)/shard_map/pallas_call | solution.py:562
  61.8 5.4 %shard_map.66 = f32[3,16,8,1,128]{4,3,2,1,0:T(1,128)S(1)} custom-call(f32[3,8,16,1,128]{4,3,2,1,0:T(1,128)S(1)} %bitcast.11), custom_call_target="tpu_custom_call" | custom-call | tf_op jit(solution)/shard_map/pallas_call | solution.py:255
  67.2 0.7 %copy.9 = f32[3,1,128,128]{3,2,1,0:T(8,128)} copy(f32[3,1,128,128]{3,2,1,0:T(8,128)S(1)} %bitcast.10) | data formatting | bytes 393216
  (1 shorter events, 0.0 us)
Async XLA Ops:
  0.0 0.9 %copy-start.3 = (f32[1,128,128]{2,1,0:T(8,128)S(1)}, f32[1,128,128]{2,1,0:T(8,128)}, u32[]{:S(2)}) copy-start(f32[1,128,128]{2,1,0:T(8,128)} %param.7) | copy-start | bytes 196612
  0.9 1.0 %copy-start = (s32[1,1,1,2,512]{4,3,2,1,0:T(2,128)S(1)}, s32[1,1,1,2,512]{4,3,2,1,0:T(2,128)}, u32[]{:S(2)}) copy-start(s32[1,1,1,2,512]{4,3,2,1,0:T(2,128)} %param.11) | copy-start | bytes 12292
  0.9 1.0 %copy-start.1 = (f32[64]{0:T(128)S(1)}, f32[64]{0:T(128)}, u32[]{:S(2)}) copy-start(f32[64]{0:T(128)} %param.9) | copy-start | bytes 772
  0.9 1.0 %copy-start.2 = (f32[64]{0:T(128)S(1)}, f32[64]{0:T(128)}, u32[]{:S(2)}) copy-start(f32[64]{0:T(128)} %param.10) | copy-start | bytes 772

commit v4 on v3

--- a/solution.py
+++ b/solution.py
@@ -55,14 +55,14 @@
     return jnp.take_along_axis(jnp.broadcast_to(values, kinds.shape), kinds, axis=1)
 
 
-def pack_atoms(raw, atoms, labels):
+def pack_atoms(raw, kinds, atoms, labels):
     stride, ranks = atoms.shape[:2]
     for group in range(stride):
         rows = pl.ds(group * ranks, ranks)
         for axis in range(3):
             atoms[group, :, axis, :] = raw[axis, rows, :] - 0.5 * cell_edge
         atoms[group, :, 3, :] = raw[3, rows, :] * charge_scale
-        labels[group, :, 0, :] = raw[4, rows, :]
+        labels[group, :, 0, :] = kinds[rows, :].astype(jnp.float32)
 
 
 def type_table(sigma, epsilon, types):
@@ -104,8 +104,9 @@
 
 
 def exchange_kernel(*refs):
-    given, (region, marks, table, types), scratch = refs[:4], refs[4:8], refs[8:]
-    held, (atoms, labels, send_own, recv_own, send_rim, recv_rim, own_sem, load_sem) = scratch[:4], scratch[4:]
+    given, outs, scratch = refs[:5], refs[5:18], refs[18:]
+    region, marks, table, types, sources, weights, edge_terms, moments, *homes, offsets, shifts = outs
+    held, (atoms, labels, send_own, recv_own, send_rim, recv_rim, own_sem, load_sem) = scratch[:5], scratch[5:]
     stride, ranks = atoms.shape[:2]
     layers = region.shape[2] - 2
     blocks = stride * ranks
@@ -117,10 +118,10 @@
     peers = list(plane_peers(spans, here))
     neighbours = list(brick_neighbours(spans, here))
     barrier, greeted = greet([p[2] for p in peers] + [n[1] for n in neighbours])
-    raw, sigma, epsilon, tiles = held
+    raw, kinds, sigma, epsilon, tiles = held
     for load in loads:
         load.wait()
-    pack_atoms(raw, atoms, labels)
+    pack_atoms(raw, kinds, atoms, labels)
     tile_table(tiles, table, blocks, layers)
     type_table(sigma, epsilon, types)
     pl.semaphore_wait(barrier, greeted)
@@ -181,12 +182,14 @@
                 )
             )
             rims[-1].start()
+    prepare_steps(offsets, shifts)
+    prepare_own(region, marks, types, sources, weights, edge_terms, moments, *homes)
     for copy in rims:
         copy.wait()
 
 
 def exchanged(given, ranks):
-    raw, _, _, tiles = given
+    raw, _, _, _, tiles = given
     blocks, width = raw.shape[1:]
     layers = blocks // (GRID * GRID)
     stride = blocks // ranks
@@ -195,6 +198,10 @@
     rim = pltpu.SemaphoreType.DMA((52,))
     vmem = pl.BlockSpec(memory_space=pltpu.VMEM)
     cells = (GRID + 2, GRID + 2, layers + 2)
+    lines = math.prod(cells)
+    entries = blocks + 4
+    single = jax.ShapeDtypeStruct((entries, ROWS, width), jnp.float32)
+    steps = jax.ShapeDtypeStruct((28, ROWS, width), jnp.float32)
     return pl.pallas_call(
         exchange_kernel,
         out_shape=(
@@ -202,9 +209,18 @@
             jax.ShapeDtypeStruct((*cells, 1, width), raw.dtype),
             jax.ShapeDtypeStruct((1, tiles.shape[1] + 2 * EDGE), jnp.int32),
             jax.ShapeDtypeStruct((ROWS, width), raw.dtype),
+            jax.ShapeDtypeStruct((lines, 10 * ROWS, width), jnp.bfloat16),
+            jax.ShapeDtypeStruct((lines, 2 * ROWS, width), jnp.bfloat16),
+            jax.ShapeDtypeStruct((lines, 4 * ROWS, width), jnp.bfloat16),
+            jax.ShapeDtypeStruct((lines, ROWS, 4 * ROWS), jnp.float32),
+            single,
+            jax.ShapeDtypeStruct((entries, 4 * ROWS, width), jnp.bfloat16),
+            single,
+            steps,
+            steps,
         ),
-        in_specs=[pl.BlockSpec(memory_space=pltpu.HBM)] * 4,
-        out_specs=(vmem,) * 4,
+        in_specs=[pl.BlockSpec(memory_space=pltpu.HBM)] * 5,
+        out_specs=(vmem,) * 13,
         scratch_shapes=[pltpu.VMEM(x.shape, x.dtype) for x in given]
         + [
             pltpu.VMEM((stride, ranks, 4, width), raw.dtype),
@@ -214,7 +230,7 @@
             rim,
             rim,
             pltpu.SemaphoreType.DMA((pieces * 2,)),
-            pltpu.SemaphoreType.DMA((4,)),
+            pltpu.SemaphoreType.DMA((5,)),
         ],
         compiler_params=pltpu.CompilerParams(
             has_side_effects=True, collective_id=0, vmem_limit_bytes=8 << 20
@@ -309,101 +325,122 @@
     return out * jnp.where(rows // 4 % 2 == 1, four, 1.0)
 
 
-def prepare_types(marks, types, sigmas, roots):
-    def one(group, carry):
-        rows = pl.ds(pl.multiple_of(group * ROWS, ROWS), ROWS)
-        kind = marks[rows, :].astype(jnp.int32)
-        sigmas[rows, :] = looked_up(types[0:1, :], kind)
-        roots[rows, :] = looked_up(types[1:2, :], kind)
-        return carry
-
-    lax.fori_loop(0, marks.shape[0] // ROWS, one, 0, unroll=15)
-
-
-def spread_row(ref, line, shape):
-    return jnp.broadcast_to(ref[pl.ds(line, 1), :], shape)
-
-
-def places(region, line):
-    block = jnp.concatenate([region[line], region[line]], axis=0)
+def places(region, at):
+    block = region[at]
+    block = jnp.concatenate([block, block], axis=0)
     return jnp.where(rows_of(block.shape) % 4 == 3, 1.0, block)
 
 
-def scaled(region, roots, line, shape):
-    charge = jnp.broadcast_to(region[line, 3:4, :], shape)
-    return jnp.where(rows_of(shape) < 4, spread_row(roots, line, shape), charge)
-
-
-def prepare_sources(region, sigmas, roots, sources, weights, moments, edge_terms):
-    shape = (ROWS, region.shape[2])
-    rows = rows_of(shape)
-    count = moments.shape[2]
-    ways = row_table([math.comb(6, k) for k in range(7)], shape)
-    edge = 1.0 / limit
-    high_at = row_table([edge**7 * math.comb(12, k) for k in range(7)], shape)
-    low_at = row_table([-(edge**4) * math.comb(6, k) for k in range(7)], shape)
-    wide_at = row_table([0.0] + [edge**7 * math.comb(12, k + 6) for k in range(1, 7)], shape)
-    near_at = jnp.where(rows == 7, inverse_powers(jnp.full(shape, limit, jnp.float32))[1], 0.0)
-    lanes = lax.broadcasted_iota(jnp.int32, (ROWS, count), 1)
-    kept = (rows_of((ROWS, count)) >= 4) == (lanes % (2 * ROWS) == 7)
-
-    def spread(line):
-        place = places(region, line)
+def type_rows(marks, types, at, shape):
+    kind = jnp.broadcast_to(marks[(*at, slice(0, 1))], shape).astype(jnp.int32)
+    return looked_up(types[0:1, :], kind), looked_up(types[1:2, :], kind)
+
+
+class Preparation:
+    def __init__(self, region, marks, types, sources, weights, edge_terms, moments):
+        self.refs = region, marks, types, sources, weights, edge_terms, moments
+        self.shape = shape = (ROWS, region.shape[-1])
+        self.rows = rows = rows_of(shape)
+        edge = 1.0 / limit
+        self.ways = row_table([math.comb(6, k) for k in range(7)], shape)
+        self.high_at = row_table([edge**7 * math.comb(12, k) for k in range(7)], shape)
+        self.low_at = row_table([-(edge**4) * math.comb(6, k) for k in range(7)], shape)
+        self.wide_at = row_table([0.0] + [edge**7 * math.comb(12, k + 6) for k in range(1, 7)], shape)
+        self.near_at = jnp.where(rows == 7, inverse_powers(jnp.full(shape, limit, jnp.float32))[1], 0.0)
+        count = moments.shape[2]
+        lanes = lax.broadcasted_iota(jnp.int32, (ROWS, count), 1)
+        self.kept = (rows_of((ROWS, count)) >= 4) == (lanes % (2 * ROWS) == 7)
+
+    def source(self, at, line):
+        region, marks, types, sources, weights, edge_terms, _ = self.refs
+        rows = self.rows
+        place = places(region, at)
+        sigma, root = type_rows(marks, types, at, self.shape)
+        charge = jnp.broadcast_to(region[(*at, slice(3, 4))], self.shape)
+        scale = jnp.where(rows < 4, root, charge)
         high, middle, low = split(place * jnp.where(rows < 4, 1.0, place))
-        sigma = spread_row(sigmas, line, shape)
         falling = rising_powers(sigma, 6 - jnp.minimum(rows, 6))
         square = sigma * sigma
-        top, rest, _ = split(ways * falling)
+        top, rest, _ = split(self.ways * falling)
         sources[line] = stacked([high, middle, high, middle, high, low, top, rest, top, rest])
-        top, rest, _ = split(place * scaled(region, roots, line, shape))
+        top, rest, _ = split(place * scale)
         weights[line] = stacked([top, rest])
-        first = split(falling * (high_at * (square * square * square) + low_at) + near_at)
-        second = split(falling * wide_at)
+        first = split(falling * (self.high_at * (square * square * square) + self.low_at) + self.near_at)
+        second = split(falling * self.wide_at)
         edge_terms[line] = stacked([first[0], second[0], first[1], second[1]])
-
-    def summed(line):
+        return place, sigma, scale
+
+    def moment(self, line):
+        _, _, _, _, weights, edge_terms, moments = self.refs
         both = lax.dot_general(
             weights[line],
             edge_terms[line],
             (((1,), (1,)), ((), ())),
             preferred_element_type=jnp.float32,
         )
-        moments[line] = jnp.where(kept, both[:ROWS] + both[ROWS:], 0.0)
-
-    lines = region.shape[0]
-    group = max(n for n in range(1, 41) if lines % n == 0)
+        moments[line] = jnp.where(self.kept, both[:ROWS] + both[ROWS:], 0.0)
+
+
+def prepare_own(region, marks, types, sources, weights, edge_terms, moments, distances, powers, scales):
+    prepared = Preparation(region, marks, types, sources, weights, edge_terms, moments)
+    rows = prepared.rows
+    layers = region.shape[2] - 2
+    column = [(y, z) for y in range(GRID) for z in range(layers)]
+
+    def line_of(x, y, z):
+        return ((x + 1) * (GRID + 2) + y + 1) * (layers + 2) + z + 1
+
+    def fill(x):
+        for k, (y, z) in enumerate(column):
+            home, sigma, scale = prepared.source((x + 1, y + 1, z + 1), line_of(x, y, z))
+            block = x * len(column) + k
+            distances[block] = jnp.where(rows < 3, -2.0 * home, jnp.where(rows % 4 < 3, 1.0, 0.0))
+            top, rest, _ = split(rising_powers(sigma, rows))
+            powers[block] = stacked([top, top, rest, rest])
+            scales[block] = 12.0 * scale
+
+    def add(x):
+        for y, z in column:
+            prepared.moment(line_of(x, y, z))
+
+    def one(x, carry):
+        add(x - 1)
+        fill(x)
+        return carry
+
+    fill(0)
+    lax.fori_loop(1, GRID, one, 0)
+    add(GRID - 1)
+    blocks = GRID * len(column)
+    distances[blocks] = jnp.zeros(distances.shape[1:], jnp.float32)
+    powers[blocks] = jnp.zeros(powers.shape[1:], powers.dtype)
+
+
+def prepare_rim(region, marks, types, sources, weights, edge_terms, moments, layers):
+    prepared = Preparation(region, marks, types, sources, weights, edge_terms, moments)
+    depth = layers + 2
+    side = (GRID + 2) * depth
+    part = -(-side // GRID)
+    inner = [y * depth + z for y in range(GRID + 2) for z in range(depth)]
+    inner = [k for k in inner if k // depth in (0, GRID + 1) or k % depth in (0, depth - 1)]
+
+    def lines(index):
+        ends = [jnp.minimum(index * part + k, side - 1) for k in range(part)]
+        far = [k + (GRID + 1) * side for k in ends]
+        return ends + far + [(index + 1) * side + k for k in inner]
 
     def one(index, carry):
-        for k in range(group):
-            summed((index - 1) * group + k)
-        for k in range(group):
-            spread(index * group + k)
+        for line in lines(index - 1):
+            prepared.moment(line)
+        for line in lines(index):
+            prepared.source((line,), line)
         return carry
 
-    for k in range(group):
-        spread(k)
-    lax.fori_loop(1, lines // group, one, 0)
-    for k in range(group):
-        summed(lines - group + k)
-
-
-def prepare_homes(region, sigmas, roots, distances, powers, scales, layers):
-    shape = distances.shape[1:]
-    rows = rows_of(shape)
-    blocks = distances.shape[0] - 1
-
-    def one(block, carry):
-        line = own_line(block, layers)
-        home = places(region, line)
-        distances[block] = jnp.where(rows < 3, -2.0 * home, jnp.where(rows % 4 < 3, 1.0, 0.0))
-        top, rest, _ = split(rising_powers(spread_row(sigmas, line, shape), rows))
-        powers[block] = stacked([top, top, rest, rest])
-        scales[block] = 12.0 * scaled(region, roots, line, shape)
-        return carry
-
-    lax.fori_loop(0, blocks, one, 0, unroll=16)
-    distances[blocks] = jnp.zeros(shape, jnp.float32)
-    powers[blocks] = jnp.zeros(powers.shape[1:], powers.dtype)
+    for line in lines(0):
+        prepared.source((line,), line)
+    lax.fori_loop(1, GRID, one, 0)
+    for line in lines(GRID - 1):
+        prepared.moment(line)
 
 
 def own_line(block, layers):
@@ -421,7 +458,7 @@
 
 
 def unpacked(pairs, index):
-    entry = pairs[index]
+    entry = pairs[0, index]
     return remainder(quotient(entry, STEPS), SHARE), quotient(entry, STEPS * SHARE), remainder(entry, STEPS)
 
 
@@ -495,17 +532,14 @@
 
 
 def force_kernel(
-    pairs, region, marks, types, out, totals, sources, weights, moments, distances, powers, scales, edges, edge_terms,
-    sigmas, roots, offsets, shifts, *slots
+    pairs, region, marks, types, _, _w, _t, _m, distances, powers, scales, offsets, shifts,
+    out, sources, weights, edge_terms, moments, totals, edges, *slots
 ):
     blocks = out.shape[1]
     layers = blocks // (GRID * GRID)
     totals[...] = jnp.zeros_like(totals)
     edges[...] = jnp.zeros_like(edges)
-    prepare_types(marks, types, sigmas, roots)
-    prepare_steps(offsets, shifts)
-    prepare_sources(region, sigmas, roots, sources, weights, moments, edge_terms)
-    prepare_homes(region, sigmas, roots, distances, powers, scales, layers)
+    prepare_rim(region, marks, types, sources, weights, edge_terms, moments, layers)
     terms, nears, strongs = [slots[k : k + BATCH] for k in range(0, 3 * BATCH, BATCH)]
 
     def step(index, carry):
@@ -528,14 +562,14 @@
             pair(t)
         return carry
 
-    groups = -(-(pairs.shape[0] - 2 * EDGE) // BATCH)
+    groups = -(-(pairs.shape[1] - 2 * EDGE) // BATCH)
     lax.fori_loop(0, groups + 2, step, 0)
 
     def finish(block, carry):
         line = own_line(block, layers)
-        place = places(region, line)
+        place = places(region, (line,))
         rows = rows_of(place.shape)
-        sigma = spread_row(sigmas, line, place.shape)
+        sigma, _ = type_rows(marks, types, (line,), place.shape)
         rising = rising_powers(sigma, rows)
         square = sigma * sigma
         first = split(jnp.where(rows == 7, 1.0, rising))
@@ -555,39 +589,25 @@
         out[axis] = totals[:blocks, axis, :]
 
 
-def brick_forces(region, marks, pairs, types, blocks):
-    lines, _, width = region.shape
-    single = pltpu.VMEM((blocks + 1, ROWS, width), jnp.float32)
-    table = pltpu.VMEM((27, ROWS, width), jnp.float32)
+def brick_forces(pairs, region, marks, types, prepared, homes, blocks):
+    width = region.shape[2]
+    entries = homes[0].shape[0]
+    vmem = pl.BlockSpec(memory_space=pltpu.VMEM)
     return pl.pallas_call(
         force_kernel,
-        out_shape=jax.ShapeDtypeStruct((3, blocks, width), jnp.float32),
-        in_specs=[
-            pl.BlockSpec(memory_space=pltpu.SMEM),
-            pl.BlockSpec(memory_space=pltpu.VMEM),
-            pl.BlockSpec(memory_space=pltpu.VMEM),
-            pl.BlockSpec(memory_space=pltpu.VMEM),
-        ],
-        out_specs=pl.BlockSpec(memory_space=pltpu.VMEM),
+        out_shape=(jax.ShapeDtypeStruct((3, blocks, width), jnp.float32),)
+        + tuple(jax.ShapeDtypeStruct(x.shape, x.dtype) for x in prepared),
+        in_specs=[pl.BlockSpec(memory_space=pltpu.SMEM)] + [vmem] * (3 + len(prepared) + len(homes)),
+        out_specs=(vmem,) * (1 + len(prepared)),
+        input_output_aliases={4 + k: 1 + k for k in range(len(prepared))},
         scratch_shapes=[
-            single,
-            pltpu.VMEM((lines, 10 * ROWS, width), jnp.bfloat16),
-            pltpu.VMEM((lines, 2 * ROWS, width), jnp.bfloat16),
-            pltpu.VMEM((lines, ROWS, 4 * ROWS), jnp.float32),
-            single,
-            pltpu.VMEM((blocks + 1, 4 * ROWS, width), jnp.bfloat16),
-            single,
-            pltpu.VMEM((blocks + 1, ROWS, 4 * ROWS), jnp.float32),
-            pltpu.VMEM((lines, 4 * ROWS, width), jnp.bfloat16),
-            pltpu.VMEM((lines, width), jnp.float32),
-            pltpu.VMEM((lines, width), jnp.float32),
-            table,
-            table,
+            pltpu.VMEM((entries, ROWS, width), jnp.float32),
+            pltpu.VMEM((entries, ROWS, 4 * ROWS), jnp.float32),
         ]
         + [pltpu.VMEM((width, 2 * width), jnp.float32)] * BATCH
         + [pltpu.VMEM((2 * width, width), jnp.bfloat16)] * (2 * BATCH),
-        compiler_params=pltpu.CompilerParams(vmem_limit_bytes=40 << 20),
-    )(pairs, region, marks, types)
+        compiler_params=pltpu.CompilerParams(vmem_limit_bytes=16 << 20),
+    )(pairs, region, marks, types, *prepared, *homes)[0]
 
 
 def per_device(coords, charges, atom_types, lj_sigma, lj_epsilon, tile_list):
@@ -596,11 +616,17 @@
     blocks = coords.shape[2]
     width = coords.shape[3]
     ranks = span_y * span_z
-    raw = jnp.concatenate([coords[:, 0], charges, atom_types.astype(coords.dtype)], axis=0)
-    given = (raw, lj_sigma[None], lj_epsilon[None], tile_list[0, 0, 0])
-    region, marks, table, types = exchanged(given, ranks)
+    raw = jnp.concatenate([coords[:, 0], charges], axis=0)
+    given = (raw, atom_types[0], lj_sigma[None], lj_epsilon[None], tile_list[0, 0, 0])
+    region, marks, table, types, *rest = exchanged(given, ranks)
     forces = brick_forces(
-        region.reshape(-1, 4, width), marks.reshape(-1, width), table.reshape(-1), types, blocks
+        table,
+        region.reshape(-1, 4, width),
+        marks.reshape(-1, 1, width),
+        types,
+        rest[:4],
+        rest[4:],
+        blocks,
     )
     return returned(forces, ranks)
 

time: 68.1 us -> 68.1 us (level)
  local copies, waits for them, and re-layouts: 0.7 us -> 3.51 us
  Pallas kernels: 65.3 us -> 63.3 us
  other arithmetic: 1.86 us -> 0.98 us
    unnamed x9, local copies, waits for them, and re-layouts: 0.7 us -> 3.51 us
    pallas_call x1, Pallas kernels: 36.7 us -> 34.9 us  [brick_forces(): pl.pallas_call(force_kernel, out_shape=(jax.ShapeDtypeStruct((3, blocks,...]
    convert_element_type x1 -> x0, other arithmetic: 0.88 us -> none  [per_device(): atom_types.astype(coords.dtype)]
where the time goes in v4:
time: 68.1 us; the launch traced here: 67.8 us
  Pallas kernels  63.3 us (93%)
  local copies, waits for them, and re-layouts  3.51 us (5%)
  other arithmetic  0.98 us (1%)
    pallas_call x1, Pallas kernels, brick_forces(): pl.pallas_call(force_kernel, out_shape=(jax.ShapeDtypeStruct((3, blocks,...  34.9 us
    pallas_call x1, Pallas kernels, exchanged(): pl.pallas_call(exchange_kernel, out_shape=(jax.ShapeDtypeStruct((*cells,...  23.1 us
    pallas_call x1, Pallas kernels, returned(): pl.pallas_call(return_kernel, out_shape=jax.ShapeDtypeStruct((axes, strid...  5.3 us
    unnamed x9, local copies, waits for them, and re-layouts  3.51 us

profile of v4, /device:TPU:0, one launch (start us, length us, event | category | flops | bytes accessed | tf_op | source)
XLA Modules:
  0.0 67.8 jit_solution(10831541601149348705)
XLA Ops:
  0.0 1.0 %pad_maximum_fusion.refs_0_ = f32[4,128,128]{2,1,0:T(8,128)S(1)} fusion(f32[1,128,128]{2,1,0:T(8,128)} %param.7, f32[3,128,128]{2,1,0:T(8,128)} %bitcast.19), kind=kLoop, calls=%fused_computation | loop fusion | flops 65536 | bytes 524288 | tf_op jit(solution)/shard_map/concatenate | solution.py:619
  1.0 0.0 copy-start
  1.0 0.8 %copy-done = s32[1,128,128]{2,1,0:T(8,128)S(1)} copy-done((s32[1,128,128]{2,1,0:T(8,128)S(1)}, s32[1,128,128]{2,1,0:T(8,128)}, u32[]{:S(2)}) %copy-start) | copy-done | bytes 65560
  1.8 0.0 copy-start.1
  1.8 0.7 %copy-done.1 = s32[1,1,1,2,512]{4,3,2,1,0:T(2,128)S(1)} copy-done((s32[1,1,1,2,512]{4,3,2,1,0:T(2,128)S(1)}, s32[1,1,1,2,512]{4,3,2,1,0:T(2,128)}, u32[]{:S(2)}) %copy-start.1) | copy-done | bytes 4120
  2.5 0.0 copy-start.2
  2.5 0.7 copy-done.2
  3.2 0.0 copy-start.3
  3.2 0.7 copy-done.3
  3.8 23.1 %shard_map.64 = (f32[6,6,10,4,128]{4,3,2,1,0:T(4,128)S(1)}, f32[6,6,10,1,128]{4,3,2,1,0:T(1,128)S(1)}, s32[1,768]{1,0:T(1,128)S(1)}, f32[8,128]{1,0:T(8,128)S(1)...) custom-call(f32[4,128,128]{2,1,0:T(8,128)S(1)} %pad_maximum_fusion.r, ...), custom_call_target="tpu_custom_call" | custom-call | tf_op jit(solution)/shard_map/pallas_call | solution.py:205
  26.9 34.9 %shard_map.65 = (f32[3,128,128]{2,1,0:T(8,128)S(1)}, bf16[360,80,128]{2,1,0:T(8,128)(2,1)S(1)}, bf16[360,16,128]{2,1,0:T(8,128)(2,1)S(1)}, bf16[360,32,128]{2,1,0:T(8,128)(2,1)S(1)}, f32[360,8,32]{2,1,0:T(8,128)S(1)}) custom-call(s32[1,768]{1,0:T(1,128)S(1)} %get-tuple-element.19.pairs, ...), custom_call_target="tpu_custom_call", output_to_operand_aliasing={{1}: (4, {}), {2}: (5, {}), {3}: (6, {}), {4}: (7, {})} | custom-call | tf_op jit(solution)/shard_map/pallas_call | solution.py:596
  61.8 5.3 %shard_map.66 = f32[3,16,8,1,128]{4,3,2,1,0:T(1,128)S(1)} custom-call(f32[3,8,16,1,128]{4,3,2,1,0:T(1,128)S(1)} %bitcast.13), custom_call_target="tpu_custom_call" | custom-call | tf_op jit(solution)/shard_map/pallas_call | solution.py:271
  67.2 0.7 %copy.17 = f32[3,1,128,128]{3,2,1,0:T(8,128)} copy(f32[3,1,128,128]{3,2,1,0:T(8,128)S(1)} %bitcast.11) | data formatting | bytes 393216
Async XLA Ops:
  1.0 0.8 %copy-start = (s32[1,128,128]{2,1,0:T(8,128)S(1)}, s32[1,128,128]{2,1,0:T(8,128)}, u32[]{:S(2)}) copy-start(s32[1,128,128]{2,1,0:T(8,128)} %param.8) | copy-start | bytes 196612
  1.8 0.7 %copy-start.1 = (s32[1,1,1,2,512]{4,3,2,1,0:T(2,128)S(1)}, s32[1,1,1,2,512]{4,3,2,1,0:T(2,128)}, u32[]{:S(2)}) copy-start(s32[1,1,1,2,512]{4,3,2,1,0:T(2,128)} %param.11) | copy-start | bytes 12292
  2.5 0.7 copy-start.2
  3.2 0.7 copy-start.3

commit v5 on v4

--- a/solution.py
+++ b/solution.py
@@ -55,20 +55,19 @@
     return jnp.take_along_axis(jnp.broadcast_to(values, kinds.shape), kinds, axis=1)
 
 
-def pack_atoms(raw, kinds, atoms, labels):
+def pack_atoms(raw, atoms, labels):
     stride, ranks = atoms.shape[:2]
     for group in range(stride):
         rows = pl.ds(group * ranks, ranks)
         for axis in range(3):
             atoms[group, :, axis, :] = raw[axis, rows, :] - 0.5 * cell_edge
         atoms[group, :, 3, :] = raw[3, rows, :] * charge_scale
-        labels[group, :, 0, :] = kinds[rows, :].astype(jnp.float32)
-
-
-def type_table(sigma, epsilon, types):
-    empty = jnp.zeros((1, types.shape[1] - sigma.shape[1]), types.dtype)
-    types[0:1, :] = jnp.concatenate([sigma[...] * sigma_scale, empty], axis=1)
-    types[1:2, :] = jnp.concatenate([jnp.sqrt(epsilon[...]), empty], axis=1)
+        labels[group, :, 0, :] = raw[4, rows, :]
+
+
+def type_table(raw, types):
+    types[0:1, :] = raw[5, 0:1, :] * sigma_scale
+    types[1:2, :] = jnp.sqrt(raw[5, 1:2, :])
 
 
 def cell_of(member, layers):
@@ -85,6 +84,7 @@
 
 def tile_table(tiles, table, blocks, layers):
     home, other = tiles[0:1, :], tiles[1:2, :]
+    width = tiles.shape[1]
     dead = home < 0
     slot = quotient(jnp.where(dead, 13 * blocks, other), blocks)
     member = remainder(jnp.where(dead, 0, other), blocks)
@@ -97,33 +97,27 @@
     there = [c + s * n for c, s, n in zip(cell_of(member, layers), steps, sizes)]
     line = ((there[0] + 1) * (GRID + 2) + there[1] + 1) * (layers + 2) + there[2] + 1
     delta = [t - o + 1 for t, o in zip(there, own)]
-    width = tiles.shape[1]
     step = (delta[0] * 3 + delta[1]) * 3 + delta[2]
     table[...] = jnp.full(table.shape, blocks * STEPS, jnp.int32)
     table[:, EDGE : EDGE + width] = (line * SHARE + jnp.where(dead, blocks, home)) * STEPS + step
 
 
 def exchange_kernel(*refs):
-    given, outs, scratch = refs[:5], refs[5:18], refs[18:]
-    region, marks, table, types, sources, weights, edge_terms, moments, *homes, offsets, shifts = outs
-    held, (atoms, labels, send_own, recv_own, send_rim, recv_rim, own_sem, load_sem) = scratch[:5], scratch[5:]
+    given, outs, scratch = refs[0], refs[1:13], refs[13:]
+    region, marks, types, sources, weights, edge_terms, moments, *homes, offsets, shifts = outs
+    raw, (atoms, labels, send_own, recv_own, send_rim, recv_rim, own_sem, load_sem) = scratch[0], scratch[1:]
     stride, ranks = atoms.shape[:2]
     layers = region.shape[2] - 2
-    blocks = stride * ranks
     spans, here = spans_of()
     me = here[1] * spans[2] + here[2]
-    loads = [pltpu.make_async_copy(src, dst, load_sem.at[k]) for k, (src, dst) in enumerate(zip(given, held))]
-    for load in loads:
-        load.start()
+    load = pltpu.make_async_copy(given, raw, load_sem.at[0])
+    load.start()
     peers = list(plane_peers(spans, here))
     neighbours = list(brick_neighbours(spans, here))
     barrier, greeted = greet([p[2] for p in peers] + [n[1] for n in neighbours])
-    raw, kinds, sigma, epsilon, tiles = held
-    for load in loads:
-        load.wait()
-    pack_atoms(raw, kinds, atoms, labels)
-    tile_table(tiles, table, blocks, layers)
-    type_table(sigma, epsilon, types)
+    load.wait()
+    pack_atoms(raw, atoms, labels)
+    type_table(raw, types)
     pl.semaphore_wait(barrier, greeted)
     chunk = math.gcd(stride, layers)
     pieces = stride // chunk
@@ -188,8 +182,7 @@
         copy.wait()
 
 
-def exchanged(given, ranks):
-    raw, _, _, _, tiles = given
+def exchanged(raw, ranks):
     blocks, width = raw.shape[1:]
     layers = blocks // (GRID * GRID)
     stride = blocks // ranks
@@ -207,7 +200,6 @@
         out_shape=(
             jax.ShapeDtypeStruct((*cells, 4, width), raw.dtype),
             jax.ShapeDtypeStruct((*cells, 1, width), raw.dtype),
-            jax.ShapeDtypeStruct((1, tiles.shape[1] + 2 * EDGE), jnp.int32),
             jax.ShapeDtypeStruct((ROWS, width), raw.dtype),
             jax.ShapeDtypeStruct((lines, 10 * ROWS, width), jnp.bfloat16),
             jax.ShapeDtypeStruct((lines, 2 * ROWS, width), jnp.bfloat16),
@@ -219,10 +211,10 @@
             steps,
             steps,
         ),
-        in_specs=[pl.BlockSpec(memory_space=pltpu.HBM)] * 5,
-        out_specs=(vmem,) * 13,
-        scratch_shapes=[pltpu.VMEM(x.shape, x.dtype) for x in given]
-        + [
+        in_specs=[pl.BlockSpec(memory_space=pltpu.HBM)],
+        out_specs=(vmem,) * 12,
+        scratch_shapes=[
+            pltpu.VMEM(raw.shape, raw.dtype),
             pltpu.VMEM((stride, ranks, 4, width), raw.dtype),
             pltpu.VMEM((stride, ranks, 1, width), raw.dtype),
             own,
@@ -230,12 +222,12 @@
             rim,
             rim,
             pltpu.SemaphoreType.DMA((pieces * 2,)),
-            pltpu.SemaphoreType.DMA((5,)),
+            pltpu.SemaphoreType.DMA((1,)),
         ],
         compiler_params=pltpu.CompilerParams(
             has_side_effects=True, collective_id=0, vmem_limit_bytes=8 << 20
         ),
-    )(*given)
+    )(raw)
 
 
 def return_kernel(forces, out, send, recv, own_sem):
@@ -532,14 +524,18 @@
 
 
 def force_kernel(
-    pairs, region, marks, types, _, _w, _t, _m, distances, powers, scales, offsets, shifts,
-    out, sources, weights, edge_terms, moments, totals, edges, *slots
+    tiles, region, marks, types, _, _w, _t, _m, distances, powers, scales, offsets, shifts,
+    out, sources, weights, edge_terms, moments, totals, edges, table, pairs, table_sem, *slots
 ):
     blocks = out.shape[1]
     layers = blocks // (GRID * GRID)
+    tile_table(tiles, table, blocks, layers)
     totals[...] = jnp.zeros_like(totals)
     edges[...] = jnp.zeros_like(edges)
+    load = pltpu.make_async_copy(table, pairs, table_sem.at[0])
+    load.start()
     prepare_rim(region, marks, types, sources, weights, edge_terms, moments, layers)
+    load.wait()
     terms, nears, strongs = [slots[k : k + BATCH] for k in range(0, 3 * BATCH, BATCH)]
 
     def step(index, carry):
@@ -589,7 +585,7 @@
         out[axis] = totals[:blocks, axis, :]
 
 
-def brick_forces(pairs, region, marks, types, prepared, homes, blocks):
+def brick_forces(tiles, region, marks, types, prepared, homes, blocks):
     width = region.shape[2]
     entries = homes[0].shape[0]
     vmem = pl.BlockSpec(memory_space=pltpu.VMEM)
@@ -597,17 +593,31 @@
         force_kernel,
         out_shape=(jax.ShapeDtypeStruct((3, blocks, width), jnp.float32),)
         + tuple(jax.ShapeDtypeStruct(x.shape, x.dtype) for x in prepared),
-        in_specs=[pl.BlockSpec(memory_space=pltpu.SMEM)] + [vmem] * (3 + len(prepared) + len(homes)),
+        in_specs=[vmem] * (4 + len(prepared) + len(homes)),
         out_specs=(vmem,) * (1 + len(prepared)),
         input_output_aliases={4 + k: 1 + k for k in range(len(prepared))},
         scratch_shapes=[
             pltpu.VMEM((entries, ROWS, width), jnp.float32),
             pltpu.VMEM((entries, ROWS, 4 * ROWS), jnp.float32),
+            pltpu.VMEM((1, tiles.shape[1] + 2 * EDGE), jnp.int32),
+            pltpu.SMEM((1, tiles.shape[1] + 2 * EDGE), jnp.int32),
+            pltpu.SemaphoreType.DMA((1,)),
         ]
         + [pltpu.VMEM((width, 2 * width), jnp.float32)] * BATCH
         + [pltpu.VMEM((2 * width, width), jnp.bfloat16)] * (2 * BATCH),
         compiler_params=pltpu.CompilerParams(vmem_limit_bytes=16 << 20),
-    )(pairs, region, marks, types, *prepared, *homes)[0]
+    )(tiles, region, marks, types, *prepared, *homes)[0]
+
+
+def joined(coords, charges, kinds, sigma, epsilon):
+    _, blocks, width = coords.shape
+
+    def put(part, slab, row=0):
+        sizes = zip((slab, row, 0), part.shape, (6, blocks, width))
+        return lax.pad(part, jnp.zeros((), part.dtype), [(low, n - low - size, 0) for low, size, n in sizes])
+
+    types = put(sigma[None, None], 5) + put(epsilon[None, None], 5, 1)
+    return put(coords, 0) + put(charges, 3) + put(kinds, 4).astype(coords.dtype) + types
 
 
 def per_device(coords, charges, atom_types, lj_sigma, lj_epsilon, tile_list):
@@ -616,11 +626,10 @@
     blocks = coords.shape[2]
     width = coords.shape[3]
     ranks = span_y * span_z
-    raw = jnp.concatenate([coords[:, 0], charges], axis=0)
-    given = (raw, atom_types[0], lj_sigma[None], lj_epsilon[None], tile_list[0, 0, 0])
-    region, marks, table, types, *rest = exchanged(given, ranks)
+    raw = joined(coords[:, 0], charges, atom_types, lj_sigma, lj_epsilon)
+    region, marks, types, *rest = exchanged(raw, ranks)
     forces = brick_forces(
-        table,
+        tile_list[0, 0, 0],
         region.reshape(-1, 4, width),
         marks.reshape(-1, 1, width),
         types,

time: 68.1 us -> 65.8 us (0.966)
  local copies, waits for them, and re-layouts: 3.51 us -> 1.36 us
    unnamed x9 -> x3, local copies, waits for them, and re-layouts: 3.51 us -> 1.36 us
    add x0 -> x1, other arithmetic: none -> 1.05 us  [joined(): put(coords, 0) + put(charges, 3) + put(kinds, 4).astype(coords.dtype)]
    concatenate x1 -> x0, other arithmetic: 0.98 us -> none  [per_device(): raw = jnp.concatenate([coords[:, 0], charges], axis=0)]
where the time goes in v5:
time: 65.8 us; the launch traced here: 65.6 us
  Pallas kernels  63.1 us (96%)
  local copies, waits for them, and re-layouts  1.36 us (2%)
  other arithmetic  1.05 us (2%)
    pallas_call x1, Pallas kernels, brick_forces(): pl.pallas_call(force_kernel, out_shape=(jax.ShapeDtypeStruct((3, blocks,...  34.6 us
    pallas_call x1, Pallas kernels, exchanged(): pl.pallas_call(exchange_kernel, out_shape=(jax.ShapeDtypeStruct((*cells,...  23.2 us
    pallas_call x1, Pallas kernels, returned(): pl.pallas_call(return_kernel, out_shape=jax.ShapeDtypeStruct((axes, strid...  5.36 us
    unnamed x3, local copies, waits for them, and re-layouts  1.36 us

profile of v5, /device:TPU:0, one launch (start us, length us, event | category | flops | bytes accessed | tf_op | source)
XLA Modules:
  0.0 65.6 jit_solution(5629203023303619600)
XLA Ops:
  0.0 1.1 %add_add_fusion.refs_0_ = f32[6,128,128]{2,1,0:T(8,128)S(1)} fusion(f32[1,1,64]{2,1,0:T(1,128)} %bitcast.16, f32[1,1,64]{2,1,0:T(1,128)} %bitcast.17, s32[1,128,128]{2,1,0:T(8,128)} %param.8, f32[1,128,128]{2,1,0:T(8,128)} %param.7, f32[3,128,128]{2,1,0:T(8,128)} %bitcast.15), kind=kLoop, calls=%fused_computation | loop fusion | flops 491520 | bytes 721408 | tf_op jit(solution)/shard_map/add | solution.py:620
  1.1 23.2 %shard_map.64 = (f32[6,6,10,4,128]{4,3,2,1,0:T(4,128)S(1)}, f32[6,6,10,1,128]{4,3,2,1,0:T(1,128)S(1)}, f32[8,128]{1,0:T(8,128)S(1)}, bf16[360,80,128]{2,1,0:T(8,...) custom-call(f32[6,128,128]{2,1,0:T(8,128)S(1)} %add_add_fusion.refs_0_), custom_call_target="tpu_custom_call" | custom-call | tf_op jit(solution)/shard_map/pallas_call | solution.py:198
  24.2 0.0 copy-start
  24.3 0.7 %copy-done = s32[1,1,1,2,512]{4,3,2,1,0:T(2,128)S(1)} copy-done((s32[1,1,1,2,512]{4,3,2,1,0:T(2,128)S(1)}, s32[1,1,1,2,512]{4,3,2,1,0:T(2,128)}, u32[]{:S(2)}) %copy-start) | copy-done | bytes 4120
  24.9 34.6 %shard_map.65 = (f32[3,128,128]{2,1,0:T(8,128)S(1)}, bf16[360,80,128]{2,1,0:T(8,128)(2,1)S(1)}, bf16[360,16,128]{2,1,0:T(8,128)(2,1)S(1)}, bf16[360,32,128]{2,1,0:T(8,128)(2,1)S(1)}, f32[360,8,32]{2,1,0:T(8,128)S(1)}) custom-call(s32[2,512]{1,0:T(2,128)S(1)} %bitcast.14, ...), custom_call_target="tpu_custom_call", output_to_operand_aliasing={{1}: (4, {}), {2}: (5, {}), {3}: (6, {}), {4}: (7, {})} | custom-call | tf_op jit(solution)/shard_map/pallas_call | solution.py:592
  59.5 5.4 %shard_map.66 = f32[3,16,8,1,128]{4,3,2,1,0:T(1,128)S(1)} custom-call(f32[3,8,16,1,128]{4,3,2,1,0:T(1,128)S(1)} %bitcast.12), custom_call_target="tpu_custom_call" | custom-call | tf_op jit(solution)/shard_map/pallas_call | solution.py:263
  64.9 0.7 %copy.17 = f32[3,1,128,128]{3,2,1,0:T(8,128)} copy(f32[3,1,128,128]{3,2,1,0:T(8,128)S(1)} %bitcast.10) | data formatting | bytes 393216
Async XLA Ops:
  24.2 0.7 %copy-start = (s32[1,1,1,2,512]{4,3,2,1,0:T(2,128)S(1)}, s32[1,1,1,2,512]{4,3,2,1,0:T(2,128)}, u32[]{:S(2)}) copy-start(s32[1,1,1,2,512]{4,3,2,1,0:T(2,128)} %param.11) | copy-start | bytes 12292

commit v6 on v5

--- a/solution.py
+++ b/solution.py
@@ -14,7 +14,9 @@
 LAG = 4
 EDGE = 128
 STEPS = 32
-SHARE = 4096
+SHARE = 1024
+LINES = 16384
+EARLY = 64
 
 cell_edge = 11.0
 cutoff = 9.0
@@ -97,15 +99,18 @@
     there = [c + s * n for c, s, n in zip(cell_of(member, layers), steps, sizes)]
     line = ((there[0] + 1) * (GRID + 2) + there[1] + 1) * (layers + 2) + there[2] + 1
     delta = [t - o + 1 for t, o in zip(there, own)]
-    step = (delta[0] * 3 + delta[1]) * 3 + delta[2]
+    step = jnp.clip((delta[0] * 3 + delta[1]) * 3 + delta[2], 0, 26)
+    line = jnp.clip(line, 0, (GRID + 2) ** 2 * (layers + 2) - 1)
+    inside = [(t >= 0) & (t < n) for t, n in zip(there, sizes)]
+    near = jnp.where(inside[0] & inside[1] & inside[2] & ~dead, LINES, 0)
     table[...] = jnp.full(table.shape, blocks * STEPS, jnp.int32)
-    table[:, EDGE : EDGE + width] = (line * SHARE + jnp.where(dead, blocks, home)) * STEPS + step
+    table[:, EDGE : EDGE + width] = ((near + line) * SHARE + jnp.where(dead, blocks, home)) * STEPS + step
 
 
 def exchange_kernel(*refs):
-    given, outs, scratch = refs[0], refs[1:13], refs[13:]
-    region, marks, types, sources, weights, edge_terms, moments, *homes, offsets, shifts = outs
-    raw, (atoms, labels, send_own, recv_own, send_rim, recv_rim, own_sem, load_sem) = scratch[0], scratch[1:]
+    (given, tiles), outs, scratch = refs[:2], refs[2:16], refs[16:]
+    region, marks, types, table, partial, sources, weights, edge_terms, moments, *homes, offsets, shifts = outs
+    (raw, pairs), (atoms, labels, send_own, recv_own, send_rim, recv_rim, own_sem, load_sem, *slots) = scratch[:2], scratch[2:]
     stride, ranks = atoms.shape[:2]
     layers = region.shape[2] - 2
     spans, here = spans_of()
@@ -117,20 +122,23 @@
     barrier, greeted = greet([p[2] for p in peers] + [n[1] for n in neighbours])
     load.wait()
     pack_atoms(raw, atoms, labels)
+    tile_table(tiles, table, stride * ranks, layers)
     type_table(raw, types)
     pl.semaphore_wait(barrier, greeted)
     chunk = math.gcd(stride, layers)
     pieces = stride // chunk
-    pairs = ((atoms, region), (labels, marks))
+    flows = ((atoms, region), (labels, marks))
 
     def place(ref, piece):
         x, y, z = cell_of(me * stride + piece * chunk, layers)
         return ref.at[x + 1, y + 1, pl.ds(z + 1, chunk)]
 
+    load = pltpu.make_async_copy(table, pairs, load_sem.at[0])
+    load.start()
     copies = []
     for hop, to, device in peers:
         for piece in range(pieces):
-            for k, (source, target) in enumerate(pairs):
+            for k, (source, target) in enumerate(flows):
                 sem = ((hop - 1) * pieces + piece) * 2 + k
                 copies.append(
                     pltpu.make_async_remote_copy(
@@ -144,7 +152,7 @@
                 )
                 copies[-1].start()
     for piece in range(pieces):
-        for k, (source, target) in enumerate(pairs):
+        for k, (source, target) in enumerate(flows):
             kept = pltpu.make_async_copy(
                 source.at[pl.ds(piece * chunk, chunk), me], place(target, piece), own_sem.at[piece * 2 + k]
             )
@@ -178,11 +186,32 @@
             rims[-1].start()
     prepare_steps(offsets, shifts)
     prepare_own(region, marks, types, sources, weights, edge_terms, moments, *homes)
+    load.wait()
+
+    def take(at, summed):
+        partial[at + 2 * BATCH] = summed
+
+    tile_loop(
+        0,
+        early_tiles(tiles.shape[1]) // BATCH,
+        pairs,
+        sources,
+        weights,
+        homes[0],
+        homes[1],
+        offsets,
+        slots,
+        take,
+    )
     for copy in rims:
         copy.wait()
 
 
-def exchanged(raw, ranks):
+def early_tiles(count):
+    return min(EARLY, count) // BATCH * BATCH
+
+
+def exchanged(raw, tiles, ranks):
     blocks, width = raw.shape[1:]
     layers = blocks // (GRID * GRID)
     stride = blocks // ranks
@@ -201,6 +230,8 @@
             jax.ShapeDtypeStruct((*cells, 4, width), raw.dtype),
             jax.ShapeDtypeStruct((*cells, 1, width), raw.dtype),
             jax.ShapeDtypeStruct((ROWS, width), raw.dtype),
+            jax.ShapeDtypeStruct((1, tiles.shape[1] + 2 * EDGE), jnp.int32),
+            jax.ShapeDtypeStruct((early_tiles(tiles.shape[1]) + 3 * BATCH, ROWS, width), jnp.float32),
             jax.ShapeDtypeStruct((lines, 10 * ROWS, width), jnp.bfloat16),
             jax.ShapeDtypeStruct((lines, 2 * ROWS, width), jnp.bfloat16),
             jax.ShapeDtypeStruct((lines, 4 * ROWS, width), jnp.bfloat16),
@@ -211,10 +242,11 @@
             steps,
             steps,
         ),
-        in_specs=[pl.BlockSpec(memory_space=pltpu.HBM)],
-        out_specs=(vmem,) * 12,
+        in_specs=[pl.BlockSpec(memory_space=pltpu.HBM), vmem],
+        out_specs=(vmem,) * 14,
         scratch_shapes=[
             pltpu.VMEM(raw.shape, raw.dtype),
+            pltpu.SMEM((1, tiles.shape[1] + 2 * EDGE), jnp.int32),
             pltpu.VMEM((stride, ranks, 4, width), raw.dtype),
             pltpu.VMEM((stride, ranks, 1, width), raw.dtype),
             own,
@@ -223,11 +255,12 @@
             rim,
             pltpu.SemaphoreType.DMA((pieces * 2,)),
             pltpu.SemaphoreType.DMA((1,)),
-        ],
+        ]
+        + tile_slots(width),
         compiler_params=pltpu.CompilerParams(
-            has_side_effects=True, collective_id=0, vmem_limit_bytes=8 << 20
+            has_side_effects=True, collective_id=0, vmem_limit_bytes=12 << 20
         ),
-    )(raw)
+    )(raw, tiles)
 
 
 def return_kernel(forces, out, send, recv, own_sem):
@@ -451,7 +484,8 @@
 
 def unpacked(pairs, index):
     entry = pairs[0, index]
-    return remainder(quotient(entry, STEPS), SHARE), quotient(entry, STEPS * SHARE), remainder(entry, STEPS)
+    line = remainder(quotient(entry, STEPS * SHARE), LINES)
+    return remainder(quotient(entry, STEPS), SHARE), line, remainder(entry, STEPS)
 
 
 def pair_terms(pairs, index, sources, distances, powers, offsets, terms):
@@ -498,8 +532,8 @@
             halves[pl.ds(width + start, 16), :] = (value - top.astype(jnp.float32)).astype(jnp.bfloat16)
 
 
-def add_forces(pairs, index, weights, moments, shifts, nears, strongs, totals, edges):
-    home, line, step = unpacked(pairs, index)
+def tile_forces(pairs, index, weights, nears, strongs):
+    _, line, _ = unpacked(pairs, index)
     left = weights[line]
     both = jnp.dot(
         jnp.concatenate([left, left], axis=1),
@@ -508,8 +542,11 @@
     )
     both = both[:ROWS] + both[ROWS:]
     width = left.shape[1]
-    rows = rows_of((ROWS, width))
-    summed = jnp.where(rows < 4, both[:, width:], both[:, :width])
+    return jnp.where(rows_of((ROWS, width)) < 4, both[:, width:], both[:, :width])
+
+
+def add_forces(summed, home, line, step, moments, shifts, totals, edges):
+    rows = rows_of(summed.shape)
     plain = jnp.where(rows < 4, summed[3:4], summed[7:8])
     shift = shifts[step]
     totals[home] += summed + shift * plain
@@ -523,43 +560,68 @@
     edges[home] += moments[line] + shift[:, :count] * plain
 
 
+def tile_loop(start, groups, pairs, sources, weights, distances, powers, offsets, slots, take):
+    terms, nears, strongs = [slots[k : k + BATCH] for k in range(0, 3 * BATCH, BATCH)]
+
+    def step(index, carry):
+        first = (index - 1) * BATCH
+
+        def push(t, lag):
+            at = first - lag + t
+            take(at, tile_forces(pairs, at + EDGE, weights, nears[t], strongs[t]))
+
+        for t in range(BATCH):
+            strengths(terms[t], nears[t], strongs[t])
+            push((t - LAG) % BATCH, BATCH if t < LAG else 0)
+            pair_terms(pairs, first + BATCH + t + EDGE, sources, distances, powers, offsets, terms[t])
+        return carry
+
+    lax.fori_loop(start, groups + 2, step, 0)
+
+
+def tile_slots(width):
+    return [pltpu.VMEM((width, 2 * width), jnp.float32)] * BATCH + [
+        pltpu.VMEM((2 * width, width), jnp.bfloat16)
+    ] * (2 * BATCH)
+
+
 def force_kernel(
-    tiles, region, marks, types, _, _w, _t, _m, distances, powers, scales, offsets, shifts,
-    out, sources, weights, edge_terms, moments, totals, edges, table, pairs, table_sem, *slots
+    table, partial, region, marks, types, _, _w, _t, _m, distances, powers, scales, offsets, shifts,
+    out, sources, weights, edge_terms, moments, totals, edges, pairs, table_sem, *slots
 ):
     blocks = out.shape[1]
     layers = blocks // (GRID * GRID)
-    tile_table(tiles, table, blocks, layers)
     totals[...] = jnp.zeros_like(totals)
     edges[...] = jnp.zeros_like(edges)
     load = pltpu.make_async_copy(table, pairs, table_sem.at[0])
     load.start()
     prepare_rim(region, marks, types, sources, weights, edge_terms, moments, layers)
     load.wait()
-    terms, nears, strongs = [slots[k : k + BATCH] for k in range(0, 3 * BATCH, BATCH)]
-
-    def step(index, carry):
-        first = (index - 1) * BATCH + EDGE
-
-        def push(t, lag):
-            add_forces(
-                pairs, first - lag + t, weights, moments, shifts, nears[t], strongs[t], totals, edges
-            )
-
-        def pull(t):
-            strengths(terms[t], nears[t], strongs[t])
-
-        def pair(t):
-            pair_terms(pairs, first + BATCH + t, sources, distances, powers, offsets, terms[t])
-
-        for t in range(BATCH):
-            pull(t)
-            push((t - LAG) % BATCH, BATCH if t < LAG else 0)
-            pair(t)
-        return carry
-
-    groups = -(-(pairs.shape[1] - 2 * EDGE) // BATCH)
-    lax.fori_loop(0, groups + 2, step, 0)
+    count = table.shape[1] - 2 * EDGE
+    early = early_tiles(count)
+
+    def merge(index, at):
+        place = early - 1 - index
+        entry = pairs[0, place + EDGE]
+        home, line, step = unpacked(pairs, place + EDGE)
+        near = quotient(entry, STEPS * SHARE * LINES)
+        summed = partial[place + 2 * BATCH]
+        add_forces(summed, jnp.where(near == 1, home, blocks), line, step, moments, shifts, totals, edges)
+        pairs[0, at + EDGE] = entry
+        return at - (1 - near)
+
+    first = lax.fori_loop(0, early, merge, jnp.int32(early - 1), unroll=4) + 1
+    for k in range(3 * BATCH):
+        pairs[0, first - 1 - k + EDGE] = blocks * STEPS
+
+    def take(at, summed):
+        home, line, step = unpacked(pairs, at + EDGE)
+        add_forces(summed, home, line, step, moments, shifts, totals, edges)
+
+    groups = -(-count // BATCH)
+    tile_loop(
+        quotient(first, BATCH), groups, pairs, sources, weights, distances, powers, offsets, slots, take
+    )
 
     def finish(block, carry):
         line = own_line(block, layers)
@@ -585,7 +647,7 @@
         out[axis] = totals[:blocks, axis, :]
 
 
-def brick_forces(tiles, region, marks, types, prepared, homes, blocks):
+def brick_forces(table, partial, region, marks, types, prepared, homes, blocks):
     width = region.shape[2]
     entries = homes[0].shape[0]
     vmem = pl.BlockSpec(memory_space=pltpu.VMEM)
@@ -593,20 +655,18 @@
         force_kernel,
         out_shape=(jax.ShapeDtypeStruct((3, blocks, width), jnp.float32),)
         + tuple(jax.ShapeDtypeStruct(x.shape, x.dtype) for x in prepared),
-        in_specs=[vmem] * (4 + len(prepared) + len(homes)),
+        in_specs=[vmem] * (5 + len(prepared) + len(homes)),
         out_specs=(vmem,) * (1 + len(prepared)),
-        input_output_aliases={4 + k: 1 + k for k in range(len(prepared))},
+        input_output_aliases={5 + k: 1 + k for k in range(len(prepared))},
         scratch_shapes=[
             pltpu.VMEM((entries, ROWS, width), jnp.float32),
             pltpu.VMEM((entries, ROWS, 4 * ROWS), jnp.float32),
-            pltpu.VMEM((1, tiles.shape[1] + 2 * EDGE), jnp.int32),
-            pltpu.SMEM((1, tiles.shape[1] + 2 * EDGE), jnp.int32),
+            pltpu.SMEM(table.shape, jnp.int32),
             pltpu.SemaphoreType.DMA((1,)),
         ]
-        + [pltpu.VMEM((width, 2 * width), jnp.float32)] * BATCH
-        + [pltpu.VMEM((2 * width, width), jnp.bfloat16)] * (2 * BATCH),
+        + tile_slots(width),
         compiler_params=pltpu.CompilerParams(vmem_limit_bytes=16 << 20),
-    )(tiles, region, marks, types, *prepared, *homes)[0]
+    )(table, partial, region, marks, types, *prepared, *homes)[0]
 
 
 def joined(coords, charges, kinds, sigma, epsilon):
@@ -627,9 +687,11 @@
     width = coords.shape[3]
     ranks = span_y * span_z
     raw = joined(coords[:, 0], charges, atom_types, lj_sigma, lj_epsilon)
-    region, marks, types, *rest = exchanged(raw, ranks)
+    tiles = tile_list[0, 0, 0]
+    region, marks, types, table, partial, *rest = exchanged(raw, tiles, ranks)
     forces = brick_forces(
-        tile_list[0, 0, 0],
+        table,
+        partial,
         region.reshape(-1, 4, width),
         marks.reshape(-1, 1, width),
         types,

time: 65.8 us -> 64.4 us (0.979)
  Pallas kernels: 63.1 us -> 61.8 us
    pallas_call x1, Pallas kernels: 34.6 us -> 33.2 us  [brick_forces(): pl.pallas_call(force_kernel, out_shape=(jax.ShapeDtypeStruct((3, blocks,...]
where the time goes in v6:
time: 64.4 us; the launch traced here: 64.3 us
  Pallas kernels  61.8 us (96%)
  local copies, waits for them, and re-layouts  1.36 us (2%)
  other arithmetic  1.05 us (2%)
    pallas_call x1, Pallas kernels, brick_forces(): pl.pallas_call(force_kernel, out_shape=(jax.ShapeDtypeStruct((3, blocks,...  33.2 us
    pallas_call x1, Pallas kernels, exchanged(): pl.pallas_call(exchange_kernel, out_shape=(jax.ShapeDtypeStruct((*cells,...  23.1 us
    pallas_call x1, Pallas kernels, returned(): pl.pallas_call(return_kernel, out_shape=jax.ShapeDtypeStruct((axes, strid...  5.46 us
    unnamed x3, local copies, waits for them, and re-layouts  1.36 us

profile of v6, /device:TPU:0, one launch (start us, length us, event | category | flops | bytes accessed | tf_op | source)
XLA Modules:
  0.0 64.3 jit_solution(13644991217173943173)
XLA Ops:
  0.0 1.1 %add_add_fusion.refs_0_ = f32[6,128,128]{2,1,0:T(8,128)S(1)} fusion(f32[1,1,64]{2,1,0:T(1,128)} %bitcast.16, f32[1,1,64]{2,1,0:T(1,128)} %bitcast.17, s32[1,128,128]{2,1,0:T(8,128)} %param.8, f32[1,128,128]{2,1,0:T(8,128)} %param.7, f32[3,128,128]{2,1,0:T(8,128)} %bitcast.15), kind=kLoop, calls=%fused_computation | loop fusion | flops 491520 | bytes 721408 | tf_op jit(solution)/shard_map/add | solution.py:680
  1.1 0.0 copy-start
  1.1 0.7 %copy-done = s32[1,1,1,2,512]{4,3,2,1,0:T(2,128)S(1)} copy-done((s32[1,1,1,2,512]{4,3,2,1,0:T(2,128)S(1)}, s32[1,1,1,2,512]{4,3,2,1,0:T(2,128)}, u32[]{:S(2)}) %copy-start) | copy-done | bytes 4120
  1.7 23.1 %shard_map.64 = (f32[6,6,10,4,128]{4,3,2,1,0:T(4,128)S(1)}, f32[6,6,10,1,128]{4,3,2,1,0:T(1,128)S(1)}, f32[8,128]{1,0:T(8,128)S(1)}, s32[1,768]{1,0:T(1,128)S(1)...) custom-call(f32[6,128,128]{2,1,0:T(8,128)S(1)} %add_add_fusion.refs_, ...), custom_call_target="tpu_custom_call" | custom-call | tf_op jit(solution)/shard_map/pallas_call | solution.py:227
  24.9 33.2 %shard_map.65 = (f32[3,128,128]{2,1,0:T(8,128)S(1)}, bf16[360,80,128]{2,1,0:T(8,128)(2,1)S(1)}, bf16[360,16,128]{2,1,0:T(8,128)(2,1)S(1)}, bf16[360,32,128]{2,1,0:T(8,128)(2,1)S(1)}, f32[360,8,32]{2,1,0:T(8,128)S(1)}) custom-call(s32[1,768]{1,0:T(1,128)S(1)} %get-tuple-element.20.table, ...), custom_call_target="tpu_custom_call", output_to_operand_aliasing={{1}: (5, {}), {2}: (6, {}), {3}: (7, {}), {4}: (8, {})} | custom-call | tf_op jit(solution)/shard_map/pallas_call | solution.py:654
  58.1 5.5 %shard_map.66 = f32[3,16,8,1,128]{4,3,2,1,0:T(1,128)S(1)} custom-call(f32[3,8,16,1,128]{4,3,2,1,0:T(1,128)S(1)} %bitcast.12), custom_call_target="tpu_custom_call" | custom-call | tf_op jit(solution)/shard_map/pallas_call | solution.py:296
  63.6 0.7 %copy.17 = f32[3,1,128,128]{3,2,1,0:T(8,128)} copy(f32[3,1,128,128]{3,2,1,0:T(8,128)S(1)} %bitcast.10) | data formatting | bytes 393216
Async XLA Ops:
  1.1 0.7 %copy-start = (s32[1,1,1,2,512]{4,3,2,1,0:T(2,128)S(1)}, s32[1,1,1,2,512]{4,3,2,1,0:T(2,128)}, u32[]{:S(2)}) copy-start(s32[1,1,1,2,512]{4,3,2,1,0:T(2,128)} %param.11) | copy-start | bytes 12292

commit v7 on v6

--- a/solution.py
+++ b/solution.py
@@ -16,7 +16,7 @@
 STEPS = 32
 SHARE = 1024
 LINES = 16384
-EARLY = 64
+EARLY = 112
 
 cell_edge = 11.0
 cutoff = 9.0
@@ -610,7 +610,7 @@
         pairs[0, at + EDGE] = entry
         return at - (1 - near)
 
-    first = lax.fori_loop(0, early, merge, jnp.int32(early - 1), unroll=4) + 1
+    first = lax.fori_loop(0, early, merge, jnp.int32(early - 1), unroll=8) + 1
     for k in range(3 * BATCH):
         pairs[0, first - 1 - k + EDGE] = blocks * STEPS
 

time: 64.4 us -> 63 us (0.978)
  Pallas kernels: 61.8 us -> 60 us
    pallas_call x1, Pallas kernels: 33.2 us -> 31.3 us  [brick_forces(): pl.pallas_call(force_kernel, out_shape=(jax.ShapeDtypeStruct((3, blocks,...]
where the time goes in v7:
time: 63 us; the launch traced here: 62.5 us
  Pallas kernels  60 us (95%)
  local copies, waits for them, and re-layouts  1.36 us (2%)
  other arithmetic  1.05 us (2%)
    pallas_call x1, Pallas kernels, brick_forces(): pl.pallas_call(force_kernel, out_shape=(jax.ShapeDtypeStruct((3, blocks,...  31.3 us
    pallas_call x1, Pallas kernels, exchanged(): pl.pallas_call(exchange_kernel, out_shape=(jax.ShapeDtypeStruct((*cells,...  23.1 us
    pallas_call x1, Pallas kernels, returned(): pl.pallas_call(return_kernel, out_shape=jax.ShapeDtypeStruct((axes, strid...  5.59 us
    unnamed x3, local copies, waits for them, and re-layouts  1.36 us

profile of v7, /device:TPU:0, one launch (start us, length us, event | category | flops | bytes accessed | tf_op | source)
XLA Modules:
  0.0 62.5 jit_solution(18031486409914683103)
XLA Ops:
  0.0 1.1 %add_add_fusion.refs_0_ = f32[6,128,128]{2,1,0:T(8,128)S(1)} fusion(f32[1,1,64]{2,1,0:T(1,128)} %bitcast.16, f32[1,1,64]{2,1,0:T(1,128)} %bitcast.17, s32[1,128,128]{2,1,0:T(8,128)} %param.8, f32[1,128,128]{2,1,0:T(8,128)} %param.7, f32[3,128,128]{2,1,0:T(8,128)} %bitcast.15), kind=kLoop, calls=%fused_computation | loop fusion | flops 491520 | bytes 721408 | tf_op jit(solution)/shard_map/add | solution.py:680
  1.1 0.0 copy-start
  1.1 0.7 %copy-done = s32[1,1,1,2,512]{4,3,2,1,0:T(2,128)S(1)} copy-done((s32[1,1,1,2,512]{4,3,2,1,0:T(2,128)S(1)}, s32[1,1,1,2,512]{4,3,2,1,0:T(2,128)}, u32[]{:S(2)}) %copy-start) | copy-done | bytes 4120
  1.7 23.1 %shard_map.64 = (f32[6,6,10,4,128]{4,3,2,1,0:T(4,128)S(1)}, f32[6,6,10,1,128]{4,3,2,1,0:T(1,128)S(1)}, f32[8,128]{1,0:T(8,128)S(1)}, s32[1,768]{1,0:T(1,128)S(1)...) custom-call(f32[6,128,128]{2,1,0:T(8,128)S(1)} %add_add_fusion.refs_, ...), custom_call_target="tpu_custom_call" | custom-call | tf_op jit(solution)/shard_map/pallas_call | solution.py:227
  24.9 31.3 %shard_map.65 = (f32[3,128,128]{2,1,0:T(8,128)S(1)}, bf16[360,80,128]{2,1,0:T(8,128)(2,1)S(1)}, bf16[360,16,128]{2,1,0:T(8,128)(2,1)S(1)}, bf16[360,32,128]{2,1,0:T(8,128)(2,1)S(1)}, f32[360,8,32]{2,1,0:T(8,128)S(1)}) custom-call(s32[1,768]{1,0:T(1,128)S(1)} %get-tuple-element.20.table, ...), custom_call_target="tpu_custom_call", output_to_operand_aliasing={{1}: (5, {}), {2}: (6, {}), {3}: (7, {}), {4}: (8, {})} | custom-call | tf_op jit(solution)/shard_map/pallas_call | solution.py:654
  56.2 5.6 %shard_map.66 = f32[3,16,8,1,128]{4,3,2,1,0:T(1,128)S(1)} custom-call(f32[3,8,16,1,128]{4,3,2,1,0:T(1,128)S(1)} %bitcast.12), custom_call_target="tpu_custom_call" | custom-call | tf_op jit(solution)/shard_map/pallas_call | solution.py:296
  61.8 0.7 %copy.17 = f32[3,1,128,128]{3,2,1,0:T(8,128)} copy(f32[3,1,128,128]{3,2,1,0:T(8,128)S(1)} %bitcast.10) | data formatting | bytes 393216
Async XLA Ops:
  1.1 0.7 %copy-start = (s32[1,1,1,2,512]{4,3,2,1,0:T(2,128)S(1)}, s32[1,1,1,2,512]{4,3,2,1,0:T(2,128)}, u32[]{:S(2)}) copy-start(s32[1,1,1,2,512]{4,3,2,1,0:T(2,128)} %param.11) | copy-start | bytes 12292
